TPU v7x, 128 devices: a whole 4x4x4 slice. The times are simulated.
128 devices in a mesh: batch: 32 (over y, z, core), mp: 4 (over x).
Axes of the slice: x: 4, y: 4, z: 4, core: 2. Of those that a mesh axis runs over, the one named last changes fastest.
Arguments:
- init_state: float32 [16384, 256], P(('batch', 'mp')), may hold values from -6 to 6
- brownian: bfloat16 [32, 16384, 256], P(None, ('batch', 'mp')), may hold values from -6 to 6
- step_size: float32 [16384], P(('batch', 'mp')), may hold values from 0.02 to 0.1
- lengths: int32 [16384], P(('batch', 'mp')), may hold values from 1 to 32, as said below
- obs_steps: int32 [16384, 8], P(('batch', 'mp')), may hold values from 1 to 32, as said below
- observed: bfloat16 [16384, 8, 128], P(('batch', 'mp')), may hold values from -6 to 6
- w_in: bfloat16 [256, 1024], P(None, 'mp'), may hold values from -0.375 to 0.375
- b_in: bfloat16 [1024], P('mp'), may hold values from -3 to 3
- w_out: bfloat16 [1024, 256], P('mp'), may hold values from -0.1875 to 0.1875
- b_out: float32 [256], replicated, may hold values from -4 to 4
- decoder: bfloat16 [256, 128], replicated, may hold values from -0.375 to 0.375
- prior_rate: float32 [256], replicated, may hold values from 0.1 to 2
- diffusion: float32 [256], replicated, may hold values from 0.7 to 1.4
Outputs:
- elbo_series: float32 [16384], P(('batch', 'mp'))
- scores: float32 [2], replicated
- grad_w_in: float32 [256, 1024], P(None, 'mp')
- grad_b_in: float32 [1024], P('mp')
- grad_w_out: float32 [1024, 256], P('mp')
- grad_b_out: float32 [256], replicated
- grad_decoder: float32 [256, 128], replicated
- grad_init: float32 [16384, 256], P(('batch', 'mp'))
Inputs may be any that keep to these rules, and one draw needn't show every extreme that they name: `lengths`: some series has 32 live steps in every draw. obs_steps[i, j] is at most lengths[i].
All inputs are finite; a program needn't handle non-finite values.
Results may differ from a plain program's by a relative error of at most 0.0019.
Values may be sent and summed in bfloat16 or wider, within the bound.
No kernel may reach another device: no remote copies, remote signals or barrier semaphores. Data moves between devices by JAX's collectives and lax.ppermute only.
A program may use at most 64 MiB of HBM per device.

v0:
```python
import functools

import jax
import jax.numpy as jnp
from jax import lax
from jax.sharding import Mesh
from jax.sharding import PartitionSpec as P

BATCH_MP = ("batch_0", "batch_1", "batch_2", "mp")
BATCH = ("batch_0", "batch_1", "batch_2")


def turned_gather(arrays, axis, dims):
    turned = [jnp.moveaxis(a, dim, 0) for a, dim in zip(arrays, dims)]
    widths = [t[0].size for t in turned]
    both = jnp.concatenate([t.reshape(-1, w) for t, w in zip(turned, widths)], axis=1)
    whole = lax.all_gather(both, axis, axis=0, tiled=True)
    blocks = jnp.split(whole, [sum(widths[:k]) for k in range(1, len(widths))], axis=1)
    return tuple(
        (
            jnp.moveaxis(b.reshape(-1, *t.shape[1:]), 0, dim)
            for b, t, dim in zip(blocks, turned, dims)
        )
    )


def by_axis(shard, axes):
    return functools.reduce(lax.psum, axes, shard)


def solve(
    init_state,
    brownian,
    step_size,
    lengths,
    obs_steps,
    observed,
    horizon,
    w_in_all,
    b_in_all,
    w_out_all,
    b_out,
    decoder,
    prior_rate,
    diffusion,
):
    row_count = init_state.shape[0]
    num_steps = brownian.shape[0]
    latent_width = init_state.shape[1]
    hidden_width = w_in_all.shape[1]
    step_col = step_size[:, None]
    root_col = jnp.sqrt(step_size)[:, None]
    bias_in = b_in_all.astype(jnp.float32)

    def forward(step_index, loop_state):
        trajectory, activities, residuals, kl_sum = loop_state
        current = lax.dynamic_index_in_dim(trajectory, step_index, 0, keepdims=False)
        increment = lax.dynamic_index_in_dim(brownian, step_index, 0, keepdims=False)
        live_now = (step_index < lengths).astype(jnp.float32)
        activity = jnp.tanh(
            jnp.dot(current.astype(jnp.bfloat16), w_in_all, preferred_element_type=jnp.float32)
            + bias_in
        ).astype(jnp.bfloat16)
        drift_now = jnp.dot(activity, w_out_all, preferred_element_type=jnp.float32) + b_out
        residual = (drift_now + prior_rate * current) / diffusion
        kl_sum = kl_sum + live_now * 0.5 * step_size * jnp.sum(residual * residual, axis=1)
        following = current + live_now[:, None] * (
            step_col * drift_now + diffusion * root_col * increment.astype(jnp.float32)
        )
        trajectory = lax.dynamic_update_index_in_dim(trajectory, following, step_index + 1, 0)
        activities = lax.dynamic_update_index_in_dim(activities, activity, step_index, 0)
        residuals = lax.dynamic_update_index_in_dim(residuals, residual, step_index, 0)
        return (trajectory, activities, residuals, kl_sum)

    start_path = lax.dynamic_update_index_in_dim(
        jnp.zeros((num_steps + 1, row_count, latent_width), jnp.float32), init_state, 0, 0
    )
    start_forward = (
        start_path,
        jnp.zeros((num_steps, row_count, hidden_width), jnp.bfloat16),
        jnp.zeros((num_steps, row_count, latent_width), jnp.float32),
        jnp.zeros((row_count,), jnp.float32),
    )
    trajectory, activities, residuals, kl_total = lax.fori_loop(0, horizon, forward, start_forward)
    picked = trajectory[obs_steps, jnp.arange(row_count, dtype=jnp.int32)[:, None]]
    picked_round = picked.astype(jnp.bfloat16).reshape(-1, latent_width)
    flat_obs = observed.reshape(-1, observed.shape[2]).astype(jnp.float32)
    misfit = jnp.dot(picked_round, decoder, preferred_element_type=jnp.float32) - flat_obs
    loglik = -0.5 * jnp.sum((misfit * misfit).reshape(row_count, -1), axis=1)
    misfit_round = misfit.astype(jnp.bfloat16)
    decoder_grad = jnp.dot(picked_round.T, misfit_round, preferred_element_type=jnp.float32)
    misfit_back = jnp.dot(misfit_round, decoder.T, preferred_element_type=jnp.float32).reshape(
        row_count, obs_steps.shape[1], latent_width
    )
    onehot = (
        obs_steps[:, :, None] == jnp.arange(num_steps + 1, dtype=jnp.int32)[None, None, :]
    ).astype(jnp.float32)
    obs_back = jnp.einsum("bjs,bjl->sbl", onehot, misfit_back, precision=lax.Precision.HIGHEST)

    def backward(back_index, loop_state):
        cotangent, sum_w_in, sum_b_in, sum_w_out, sum_b_out = loop_state
        step_index = horizon - 1 - back_index
        current = lax.dynamic_index_in_dim(trajectory, step_index, 0, keepdims=False)
        activity = lax.dynamic_index_in_dim(activities, step_index, 0, keepdims=False)
        residual = lax.dynamic_index_in_dim(residuals, step_index, 0, keepdims=False)
        obs_here = lax.dynamic_index_in_dim(obs_back, step_index, 0, keepdims=False)
        live_now = (step_index < lengths).astype(jnp.float32)
        factor = (live_now * step_size)[:, None]
        scaled = residual / diffusion
        update = factor * (cotangent + scaled)
        update_round = update.astype(jnp.bfloat16)
        activity_value = activity.astype(jnp.float32)
        pre_grad = jnp.dot(update_round, w_out_all.T, preferred_element_type=jnp.float32) * (
            1.0 - activity_value * activity_value
        )
        pre_round = pre_grad.astype(jnp.bfloat16)
        cotangent = (
            cotangent
            + factor * prior_rate * scaled
            + jnp.dot(pre_round, w_in_all.T, preferred_element_type=jnp.float32)
            + obs_here
        )
        sum_w_in = sum_w_in + jnp.dot(
            current.astype(jnp.bfloat16).T, pre_round, preferred_element_type=jnp.float32
        )
        sum_b_in = sum_b_in + jnp.sum(pre_grad, axis=0)
        sum_w_out = sum_w_out + jnp.dot(
            activity.T, update_round, preferred_element_type=jnp.float32
        )
        sum_b_out = sum_b_out + jnp.sum(update, axis=0)
        return (cotangent, sum_w_in, sum_b_in, sum_w_out, sum_b_out)

    start_back = (
        lax.dynamic_index_in_dim(obs_back, horizon, 0, keepdims=False),
        jnp.zeros((latent_width, hidden_width), jnp.float32),
        jnp.zeros((hidden_width,), jnp.float32),
        jnp.zeros((hidden_width, latent_width), jnp.float32),
        jnp.zeros((latent_width,), jnp.float32),
    )
    cotangent, sum_w_in, sum_b_in, sum_w_out, sum_b_out = lax.fori_loop(
        0, horizon, backward, start_back
    )
    divisor = (latent_width * lengths + observed.shape[2] * obs_steps.shape[1]).astype(jnp.float32)
    elbo_rows = (loglik - kl_total) / divisor
    return (
        elbo_rows,
        cotangent,
        jnp.sum(loglik),
        jnp.sum(kl_total),
        sum_w_in,
        sum_b_in,
        sum_w_out,
        sum_b_out,
        decoder_grad,
    )


def on_device(
    init_state,
    brownian,
    step_size,
    lengths,
    obs_steps,
    observed,
    w_in,
    b_in,
    w_out,
    b_out,
    decoder,
    prior_rate,
    diffusion,
):
    w_in_all, w_out_all, b_in_all = turned_gather((w_in, w_out, b_in), "mp", (1, 0, 0))
    row_count = init_state.shape[0]
    num_steps = brownian.shape[0]
    hidden_width = w_in_all.shape[1]
    shared = (w_in_all, b_in_all, w_out_all, b_out, decoder, prior_rate, diffusion)
    outcome = solve(
        init_state, brownian, step_size, lengths, obs_steps, observed, num_steps, *shared
    )
    (
        elbo_series,
        cotangent,
        loglik_local,
        kl_local,
        sum_w_in,
        sum_b_in,
        sum_w_out,
        sum_b_out,
        decoder_grad,
    ) = outcome
    loglik_all, kl_all = (by_axis(loglik_local, BATCH_MP), by_axis(kl_local, BATCH_MP))
    total_series = row_count * lax.axis_size(BATCH) * lax.axis_size("mp")
    share = hidden_width // lax.axis_size("mp")
    offset = lax.axis_index("mp") * share
    all_w_in, all_b_in, all_w_out, all_b_out, all_decoder = lax.psum(
        (sum_w_in, sum_b_in, sum_w_out, sum_b_out, decoder_grad), BATCH_MP
    )
    own_w_in = lax.dynamic_slice_in_dim(all_w_in, offset, share, 1)
    own_b_in = lax.dynamic_slice_in_dim(all_b_in, offset, share, 0)
    own_w_out = lax.dynamic_slice_in_dim(all_w_out, offset, share, 0)
    scores = jnp.stack([loglik_all / total_series, kl_all / total_series])
    return (
        elbo_series,
        scores,
        own_w_in / total_series,
        own_b_in / total_series,
        own_w_out / total_series,
        all_b_out / total_series,
        all_decoder / total_series,
        cotangent,
    )


def solution(mesh):
    torus = Mesh(
        mesh.devices.reshape(4, 4, 2, mesh.shape["mp"]), ("batch_0", "batch_1", "batch_2", "mp")
    )
    placed = (
        P(BATCH_MP, None),
        P(None, BATCH_MP, None),
        P(BATCH_MP),
        P(BATCH_MP),
        P(BATCH_MP, None),
        P(BATCH_MP, None, None),
        P(None, "mp"),
        P("mp"),
        P("mp", None),
        P(),
        P(),
        P(),
        P(),
    )
    return jax.shard_map(
        on_device,
        mesh=torus,
        in_specs=placed,
        out_specs=(
            P(BATCH_MP),
            P(),
            P(None, "mp"),
            P("mp"),
            P("mp", None),
            P(),
            P(),
            P(BATCH_MP, None),
        ),
        check_vma=False,
    )
```

profile of v0, /device:TPU:1, one launch (start us, length us, event | category | flops | bytes accessed | tf_op | source)
XLA Modules:
  0.0 789.1 jit_solution(2459899260719976224)
XLA Ops:
  14.5 3.5 dynamic_update_slice.37
  18.0 19.7 %all-gather.2.cloned.1.call-done = bf16[1024,513]{1,0:T(8,128)(2,1)} async-done(((bf16[256,513]{1,0:T(8,128)(2,1)}), bf16[1024,513]{1,0:T(8,128)(2,1)}) %all-gather.2.cloned.1.call-update) | async-done | bytes 1050640 | tf_op jit(solution)/shard_map/all_gather | solution.py:17
  37.7 2.3 fusion.37
  42.4 313.4 %while.46 = (s32[]{:T(128)}, f32[33,128,256]{2,1,0:T(8,128)}, bf16[32,128,1024]{2,1,0:T(8,128)(2,1)}, f32[32,128,256]{2,1,0:T(8,128)}, f32[128]{0:T(128)S(1)}, /...) while((s32[]{:T(128)}, f32[33,128,256]{2,1,0:T(8,128)}, ...), condition=%wide.region_2.3_spmd.clone, body=%wide.region_0.2_spmd.clone.sunk | while | flops 135005056 | bytes 20398324 | solution.py:84
  45.2 2.2 copy.44
  55.0 2.2 copy.44
  64.8 2.2 copy.44
  74.6 2.2 copy.44
  84.4 2.2 copy.44
  94.2 2.2 copy.44
  123.6 2.2 copy.44
  152.9 2.2 copy.44
  182.3 2.2 copy.44
  355.8 3.9 convert.37
  359.7 12.7 %gather_fusion = bf16[1024,256]{1,0:T(8,128)(2,1)S(1)} fusion(f32[33,128,256]{2,1,0:T(8,128)} %get-tuple-element.970, s32[1024]{0:T(1024)S(1)} %reshape.71), kind=kCustom, calls=%fused_computation | custom fusion | bytes 1056768 | tf_op jit(solution)/shard_map/gather | solution.py:85
  375.1 2.9 fusion.23
  378.1 2.3 copy-done.3
  380.3 242.8 %while.47 = (s32[]{:T(128)}, f32[128,256]{1,0:T(8,128)S(1)}, f32[256,1024]{1,0:T(8,128)S(1)}, f32[1024]{0:T(1024)S(1)}, f32[1024,256]{1,0:T(8,128)S(1)}, /*index...) while((s32[]{:T(128)}, f32[128,256]{1,0:T(8,128)S(1)}, ...), condition=%wide.region_18.19_spmd.clone, body=%wide.region_15.18_spmd.clone.sunk | while | flops 270632448 | bytes 9987913 | solution.py:140
  625.8 8.7 %all-reduce.5 = (f32[]{:T(128)}, f32[]{:T(128)}) all-reduce(f32[]{:T(128)} %get-tuple-element.1030, f32[]{:T(128)} %get-tuple-element.1028), channel_id=1, replica_groups=mesh['batch_0'=4,'batch_1'=4,'batch_2'=2,'mp'=4] {'batch_0'}, use_global_device_ids=true, to_apply=%region_11.12 | all-reduce | flops 2 | bytes 16 | tf_op jit(solution)/shard_map/psum | solution.py:28
  634.5 9.7 %all-reduce.4 = (f32[]{:T(128)}, f32[]{:T(128)}) all-reduce(f32[]{:T(128)} %get-tuple-element.1012, f32[]{:T(128)} %get-tuple-element.1013), channel_id=1, replica_groups=mesh['batch_0'=4,'batch_1'=4,'batch_2'=2,'mp'=4] {'batch_1'}, use_global_device_ids=true, to_apply=%region_12.13 | all-reduce | flops 2 | bytes 16 | tf_op jit(solution)/shard_map/psum | solution.py:28
  644.2 8.4 %all-reduce.6 = (f32[]{:T(128)}, f32[]{:T(128)}) all-reduce(f32[]{:T(128)} %get-tuple-element.1010, f32[]{:T(128)} %get-tuple-element.1011), channel_id=1, replica_groups=mesh['batch_0'=4,'batch_1'=4,'batch_2'=2,'mp'=4] {'batch_2'}, use_global_device_ids=true, to_apply=%region_13.14 | all-reduce | flops 2 | bytes 16 | tf_op jit(solution)/shard_map/psum | solution.py:28
  652.6 8.2 %all-reduce.3 = (f32[]{:T(128)}, f32[]{:T(128)}) all-reduce(f32[]{:T(128)} %get-tuple-element.1014, f32[]{:T(128)} %get-tuple-element.1015), channel_id=1, replica_groups=mesh['batch_0'=4,'batch_1'=4,'batch_2'=2,'mp'=4] {'mp'}, use_global_device_ids=true, to_apply=%region_14.15 | all-reduce | flops 2 | bytes 16 | tf_op jit(solution)/shard_map/psum | solution.py:28
  662.1 64.4 %all-reduce.1 = (f32[1024]{0:T(1024)S(1)}, f32[256]{0:T(256)S(1)}) all-reduce(f32[1024]{0:T(1024)S(1)} %get-tuple-element.769, f32[256]{0:T(256)S(1)} %get-tuple-element.771), channel_id=1, replica_groups=mesh['batch_0'=4,'batch_1'=4,'batch_2'=2,'mp'=4] {'batch_0','batch_1','b..., use_global_device_ids=true, to_apply=%region_20.21 | all-reduce | flops 1280 | bytes 10240 | tf_op jit(solution)/shard_map/psum | solution.py:196
  727.8 51.0 %all-reduce.9.cloned.1.call-done = (f32[256,1024]{1,0:T(8,128)}, f32[1024,256]{1,0:T(8,128)}, f32[256,128]{1,0:T(8,128)}) async-done(((f32[256,1024]{1,0:T(8,128)}, f32[1024,256]{1,0:T(8,128)}, f32[256,128]{1,0:T(8,128)}), (f32[256,1024]{1,0:T(8,128)}, f32[1024,256]{1,0:T(8,128)}, f32[256,128]{1,0:T(8,128)})) %all-reduce.9.cloned.1.call-update) | async-done | bytes 2228240 | tf_op jit(solution)/shard_map/psum | solution.py:196
  (653 shorter events, 551.9 us)
Async XLA Ops:
  7.2 365.2 %copy-start = (bf16[256,128]{1,0:T(8,128)(2,1)S(1)}, bf16[256,128]{1,0:T(8,128)(2,1)}, u32[]{:S(2)}) copy-start(bf16[256,128]{1,0:T(8,128)(2,1)} %param.27) | copy-start | bytes 196612
  7.2 10.8 %copy-start.8 = (f32[128]{0:T(128)S(1)}, f32[128]{0:T(128)}, u32[]{:S(2)}) copy-start(f32[128]{0:T(128)} %param.19) | copy-start | bytes 1540
  7.2 30.5 %all-gather.2.cloned.1.call-start = ((), (), s32[]{:S(2)}) async-start(), calls=%async_computation | async-start | bytes 1638400 | tf_op jit(solution)/shard_map/all_gather | solution.py:17
  10.7 768.1 %all-reduce.9.cloned.1.call-start = ((), (), s32[]{:S(2)}) async-start(), calls=%async_computation.1 | async-start | bytes 4456448 | tf_op jit(solution)/shard_map/psum | solution.py:196
  14.5 27.8 %copy-start.6 = (f32[256]{0:T(256)S(1)}, f32[256]{0:T(256)}, u32[]{:S(2)}) copy-start(f32[256]{0:T(256)} %param.29) | copy-start | bytes 3076
  14.5 27.8 %copy-start.7 = (s32[128]{0:T(128)S(1)}, s32[128]{0:T(128)}, u32[]{:S(2)}) copy-start(s32[128]{0:T(128)} %param.20) | copy-start | bytes 1540
  14.5 27.9 %copy-start.9 = (f32[256]{0:T(256)S(1)}, f32[256]{0:T(256)}, u32[]{:S(2)}) copy-start(f32[256]{0:T(256)} %param.28) | copy-start | bytes 3076
  14.5 27.9 %copy-start.10 = (f32[256]{0:T(256)S(1)}, f32[256]{0:T(256)}, u32[]{:S(2)}) copy-start(f32[256]{0:T(256)} %param.26) | copy-start | bytes 3076
  405.4 4.0 copy-start.5
  413.0 4.0 copy-start.5
  420.6 4.0 copy-start.5
  428.2 4.0 copy-start.5
  435.7 4.0 copy-start.5
  443.3 4.0 copy-start.5
  450.9 4.0 copy-start.5
  458.5 4.0 copy-start.5
  466.1 4.0 copy-start.5
  473.7 4.0 copy-start.5
  481.3 4.0 copy-start.5
  488.8 4.0 copy-start.5
  496.4 4.0 copy-start.5
  549.5 4.0 copy-start.5
  602.7 4.0 copy-start.5
  623.1 159.1 %copy-start.4 = (f32[128,256]{1,0:T(8,128)}, f32[128,256]{1,0:T(8,128)S(1)}, u32[]{:S(2)}) copy-start(f32[128,256]{1,0:T(8,128)S(1)} %get-tuple-element.763) | copy-start | bytes 393220
  (20 other events, 73.4 us)
Sparse Core Ops, SparseCore 0:
  10.8 26.8 all-gather.1
  624.5 154.2 all-reduce.8
where the time goes:
time: 799 us; the launch traced here: 789 us
  matrix products  284 us (36%)
  local copies, waits for them, and re-layouts  235 us (29%)
  blocking collectives  99.5 us (12%)
  other arithmetic  80.4 us (10%)
  waiting for transfers between devices  70.8 us (9%)
  between operations  15.6 us (2%)
    while x128, local copies, waits for them, and re-layouts  136 us
    psum x1, blocking collectives, on_device(): lax.psum((sum_w_in, sum_b_in, sum_w_out, sum_b_out, decoder_grad), BATCH_MP)  64.4 us
    dot_general x32, matrix products, forward(): jnp.dot(current.astype(jnp.bfloat16), w_in_all, preferred_element_type=jn...  59.4 us
    dot_general x32, matrix products, forward(): jnp.dot(activity, w_out_all, preferred_element_type=jnp.float32) + b_out  55.5 us
    psum x1, waiting for transfers between devices, on_device(): lax.psum((sum_w_in, sum_b_in, sum_w_out, sum_b_out, decoder_grad), BATCH_MP)  51 us
    dot_general x32, matrix products, backward(): jnp.dot(activity.T, update_round, preferred_element_type=jnp.float32)  44.8 us
    dynamic_slice x32, local copies, waits for them, and re-layouts, backward(): obs_here = lax.dynamic_index_in_dim(obs_back, step_index, 0, keepdims=False)  42.4 us
    dot_general x32, matrix products, backward(): jnp.dot(current.astype(jnp.bfloat16).T, pre_round, preferred_element_type...  41.2 us
  transfers between devices with their start and end apart: 2, of which 2 were waited for; matrix products, arithmetic and copies ran while one was open for 1% of the time, Pallas kernels for 0%

commit v1 on v0

v1 whole, which is shorter than its diff:
```python
import functools

import jax
import jax.numpy as jnp
from jax import lax
from jax.experimental import pallas as pl
from jax.experimental.pallas import tpu as pltpu

F32 = jnp.float32
BF16 = jnp.bfloat16


def wide(x):
    return jnp.concatenate([x, x], axis=1)


def column(row, rows):
    return jnp.transpose(jnp.broadcast_to(row, (rows, rows)))


def series_kernel(
    init,
    brown,
    step,
    lens,
    obs_steps,
    obs,
    w_in,
    b_in,
    w_out,
    b_out,
    dec,
    prior,
    diff,
    grads,
    dec_grad,
    in_bias,
    out_bias,
    sums,
    elbo,
    grad_init,
    act,
    pg,
    low,
    upd,
    scaled,
    w_in_t,
    w_out_t,
    obs_at,
    state,
    kl_acc,
    sq_acc,
    in_acc,
    out_acc,
    acc_in,
    acc_out,
):
    steps, rows, width = brown.shape
    parts = w_in.shape[0]
    share = w_in.shape[2]
    hidden = parts * share
    cols = dec.shape[1]
    seen = obs.shape[0]

    step_b = column(step[...], rows)
    root_b = jnp.sqrt(step_b)
    lens_b = column(lens[...], rows)
    inv = 1.0 / diff[...]
    for j in range(seen):
        obs_at[j] = jnp.broadcast_to(obs_steps[:, j : j + 1], (rows, cols))
    for q in range(parts):
        w_out_t[q] = jnp.transpose(w_out[q])
        w_in_t[q * share : (q + 1) * share, :] = jnp.transpose(w_in[q])
    dec_t = jnp.transpose(dec[...])
    w_in_t[hidden : hidden + cols, :] = dec_t
    w_in_t[hidden + cols : hidden + 2 * cols, :] = dec_t

    state[...] = init[...]
    kl_acc[...] = jnp.zeros_like(kl_acc)
    sq_acc[...] = jnp.zeros_like(sq_acc)
    in_acc[...] = jnp.zeros_like(in_acc)
    out_acc[...] = jnp.zeros_like(out_acc)
    acc_in[...] = jnp.zeros_like(acc_in)
    acc_out[...] = jnp.zeros_like(acc_out)

    def observe(k, low_now):
        seen_now = jnp.dot(low_now, dec[...], preferred_element_type=F32)
        total = jnp.zeros((rows, cols), F32)
        squares = sq_acc[...]
        for j in range(seen):
            misfit = jnp.where(obs_at[j] == k, seen_now - obs[j].astype(F32), 0.0)
            squares = squares + misfit * misfit
            total = total + misfit.astype(BF16).astype(F32)
        sq_acc[...] = squares
        high = total.astype(BF16)
        pg[k, :, hidden : hidden + cols] = high
        pg[k, :, hidden + cols : hidden + 2 * cols] = (total - high.astype(F32)).astype(BF16)

    def forward(k, _):
        now = state[...]
        low_now = now.astype(BF16)
        low[k] = low_now
        for q in range(parts):
            block = slice(q * share, (q + 1) * share)
            pre = jnp.dot(low_now, w_in[q], preferred_element_type=F32) + b_in[:, block]
            act[k, :, block] = jnp.tanh(pre).astype(BF16)
        observe(k, low_now)
        drift = (
            jnp.dot(act[k], w_out[...].reshape(hidden, width), preferred_element_type=F32)
            + b_out[...]
        )
        live = k < lens_b
        factor = wide(jnp.where(live, step_b, 0.0))
        noise = wide(jnp.where(live, root_b, 0.0))
        residual = (drift + prior[...] * now) * inv
        scaled[k] = residual * inv
        spent = factor * (residual * residual)
        kl_acc[...] += spent[:, :rows] + spent[:, rows:]
        state[...] = now + (factor * drift + diff[...] * noise * brown[k].astype(F32))
        return 0

    lax.fori_loop(0, steps, forward, 0)
    last = state[...].astype(BF16)
    low[steps] = last
    observe(steps, last)

    state[...] = jnp.dot(
        pg[steps, :, hidden:], w_in_t[hidden:, :], preferred_element_type=F32
    )

    def backward(i, _):
        k = steps - 1 - i
        cot = state[...]
        factor = wide(jnp.where(k < lens_b, step_b, 0.0))
        pull = scaled[k]
        update = factor * (cot + pull)
        low_up = update.astype(BF16)
        upd[k] = low_up
        out_acc[...] += jnp.sum(update.reshape(rows // 8, 8, width), axis=0)
        for q in range(parts):
            block = slice(q * share, (q + 1) * share)
            a = act[k, :, block].astype(F32)
            pre = jnp.dot(low_up, w_out_t[q], preferred_element_type=F32) * (1.0 - a * a)
            pg[k, :, block] = pre.astype(BF16)
            in_acc[:, block] += jnp.sum(pre.reshape(rows // 8, 8, share), axis=0)
        state[...] = (
            cot
            + factor * (prior[...] * pull)
            + jnp.dot(pg[k], w_in_t[...], preferred_element_type=F32)
        )
        return 0

    lax.fori_loop(0, steps, backward, 0)
    grad_init[...] = state[...]

    chunk = 4
    turned = (((0,), (0,)), ((), ()))

    def gather_grads(i, _):
        at = pl.ds(i * chunk, chunk)
        acc_in[...] += lax.dot_general(
            low[at].reshape(chunk * rows, width),
            pg[at].reshape(chunk * rows, hidden + 2 * cols),
            turned,
            preferred_element_type=F32,
        )
        acc_out[...] += lax.dot_general(
            upd[at].reshape(chunk * rows, width),
            act[at].reshape(chunk * rows, hidden),
            turned,
            preferred_element_type=F32,
        )
        return 0

    lax.fori_loop(0, steps // chunk, gather_grads, 0)
    final = acc_in[:, hidden:] + lax.dot_general(
        low[steps], pg[steps, :, hidden:], turned, preferred_element_type=F32
    )
    dec_grad[...] = final[:, :cols] + final[:, cols:]
    for q in range(parts):
        block = slice(q * share, (q + 1) * share)
        grads[q, :width, :] = acc_in[:, block]
        grads[q, width:, :] = acc_out[:, block]
    in_bias[...] = jnp.sum(in_acc[...], axis=0, keepdims=True)
    out_bias[...] = jnp.sum(out_acc[...], axis=0, keepdims=True)

    kl = 0.5 * jnp.sum(jnp.transpose(kl_acc[...]), axis=0, keepdims=True)
    loglik = -0.5 * jnp.sum(jnp.transpose(sq_acc[...]), axis=0, keepdims=True)
    sums[0:1, :] = loglik
    sums[1:2, :] = kl
    divisor = (width * lens[...] + cols * seen).astype(F32)
    elbo[...] = (loglik - kl) / divisor


def solve(init, brown, step, lengths, obs_steps, observed, w_in, b_in, w_out, b_out, dec, prior, diff):
    rows, width = init.shape
    steps = brown.shape[0]
    parts, _, share = w_in.shape
    hidden = parts * share
    seen, cols = observed.shape[1:]
    vmem = pl.BlockSpec(memory_space=pltpu.VMEM)
    shape = jax.ShapeDtypeStruct
    outs = (
        shape((parts, 2 * width, share), F32),
        shape((width, cols), F32),
        shape((1, hidden), F32),
        shape((1, width), F32),
        shape((2, rows), F32),
        shape((1, rows), F32),
        shape((rows, width), F32),
    )
    return pl.pallas_call(
        series_kernel,
        name="series",
        out_shape=outs,
        in_specs=[vmem] * 13,
        out_specs=(vmem,) * len(outs),
        scratch_shapes=[
            pltpu.VMEM((steps, rows, hidden), BF16),
            pltpu.VMEM((steps + 1, rows, hidden + 2 * cols), BF16),
            pltpu.VMEM((steps + 1, rows, width), BF16),
            pltpu.VMEM((steps, rows, width), BF16),
            pltpu.VMEM((steps, rows, width), F32),
            pltpu.VMEM((hidden + 2 * cols, width), BF16),
            pltpu.VMEM((parts, width, share), BF16),
            pltpu.VMEM((seen, rows, cols), jnp.int32),
            pltpu.VMEM((rows, width), F32),
            pltpu.VMEM((rows, rows), F32),
            pltpu.VMEM((rows, cols), F32),
            pltpu.VMEM((8, hidden), F32),
            pltpu.VMEM((8, width), F32),
            pltpu.VMEM((width, hidden + 2 * cols), F32),
            pltpu.VMEM((width, hidden), F32),
        ],
        compiler_params=pltpu.CompilerParams(vmem_limit_bytes=60 * 1024 * 1024),
        cost_estimate=pl.CostEstimate(
            flops=12 * steps * rows * width * hidden,
            bytes_accessed=8 * 1024 * 1024,
            transcendentals=steps * rows * hidden,
        ),
    )(
        init,
        brown,
        step[None],
        lengths[None],
        obs_steps,
        jnp.transpose(observed, (1, 0, 2)),
        w_in,
        b_in,
        w_out,
        b_out[None],
        dec,
        prior[None],
        diff[None],
    )


AXES = ("batch", "mp")


def on_device(
    init_state,
    brownian,
    step_size,
    lengths,
    obs_steps,
    observed,
    w_in,
    b_in,
    w_out,
    b_out,
    decoder,
    prior_rate,
    diffusion,
):
    w_in_all = lax.all_gather(w_in, "mp", axis=0)
    w_out_all = lax.all_gather(w_out, "mp", axis=0)
    b_in_all = lax.all_gather(b_in, "mp", axis=0, tiled=True).astype(F32)[None]
    grads, dec_grad, in_bias, out_bias, sums, elbo, grad_init = solve(
        init_state,
        brownian,
        step_size,
        lengths,
        obs_steps,
        observed,
        w_in_all,
        b_in_all,
        w_out_all,
        b_out,
        decoder,
        prior_rate,
        diffusion,
    )
    total = init_state.shape[0] * lax.axis_size("batch") * lax.axis_size("mp")
    width = init_state.shape[1]
    share = w_in.shape[1]
    hidden = share * lax.axis_size("mp")
    own = lax.psum_scatter(grads, "mp", scatter_dimension=0)
    own = lax.psum(own, "batch") / total
    flat = jnp.concatenate(
        [dec_grad.reshape(-1), in_bias.reshape(-1), out_bias.reshape(-1), jnp.sum(sums, axis=1)]
    )
    flat = lax.psum(flat, AXES) / total
    size = dec_grad.size
    all_in_bias = flat[size : size + hidden]
    own_in_bias = lax.dynamic_slice_in_dim(all_in_bias, lax.axis_index("mp") * share, share, 0)
    return (
        elbo.reshape(-1),
        flat[size + hidden + width :],
        own[:width],
        own_in_bias,
        own[width:].T,
        flat[size + hidden : size + hidden + width],
        flat[:size].reshape(dec_grad.shape),
        grad_init,
    )


def solution(mesh):
    from jax.sharding import PartitionSpec as P

    return jax.shard_map(
        on_device,
        mesh=mesh,
        in_specs=(
            P(AXES, None),
            P(None, AXES, None),
            P(AXES),
            P(AXES),
            P(AXES, None),
            P(AXES, None, None),
            P(None, "mp"),
            P("mp"),
            P("mp", None),
            P(),
            P(),
            P(),
            P(),
        ),
        out_specs=(
            P(AXES),
            P(),
            P(None, "mp"),
            P("mp"),
            P("mp", None),
            P(),
            P(),
            P(AXES, None),
        ),
        check_vma=False,
    )
```

time: 799 us -> 360 us (0.45); the launches traced: 789 us -> 360 us
  matrix products: 284 us -> 0 us
  local copies, waits for them, and re-layouts: 235 us -> 8.41 us
  waiting for transfers between devices: 70.8 us -> 261 us
  other arithmetic: 80.4 us -> 3.36 us
  blocking collectives: 99.5 us -> 30.6 us
  Pallas kernels: 0 us -> 40.6 us
    dot_general x196 -> x0, matrix products: 284 us -> none  [the longest x32 59.4 us: forward(): jnp.dot(current.astype(jnp.bfloat16), w_in_all, preferred_element_type=jn...]
    psum x1 -> x2, waiting for transfers between devices: 51 us -> 225 us  [the longest x1 124 us: on_device(): flat = lax.psum(flat, AXES) / total]
    while x128 -> x0, local copies, waits for them, and re-layouts: 136 us -> none
    psum x5 -> x0, blocking collectives: 99.5 us -> none  [the longest x1 64.4 us: on_device(): lax.psum((sum_w_in, sum_b_in, sum_w_out, sum_b_out, decoder_grad), BATCH_MP)]
    dynamic_slice x64 -> x1, local copies, waits for them, and re-layouts: 71.6 us -> 0.63 us  [on_device(): lax.dynamic_slice_in_dim(all_in_bias, lax.axis_index('mp') * share, share...]
    reduce_sum x66 -> x1, other arithmetic: 66.1 us -> 0.12 us  [on_device(): jnp.sum(sums, axis=1)]
    pallas_call x0 -> x1, Pallas kernels: none -> 40.6 us  [solve(): pl.pallas_call(series_kernel, name='series', out_shape=outs, in_specs=[vm...]
    reduce_scatter x0 -> x1, waiting for transfers between devices: none -> 35.8 us  [on_device(): own = lax.psum_scatter(grads, 'mp', scatter_dimension=0)]
  transfers between devices with their start and end apart: 2 -> 3, of which waited for: 2 -> 3; matrix products, arithmetic and copies ran while one was open for 1% -> 1% of each run, Pallas kernels for 0% -> 0%
where the time goes in v1:
time: 360 us
  waiting for transfers between devices  261 us (72%)
  Pallas kernels  40.6 us (11%)
  blocking collectives  30.6 us (8%)
  between operations  15.5 us (4%)
  local copies, waits for them, and re-layouts  8.41 us (2%)
    psum x1, waiting for transfers between devices, on_device(): flat = lax.psum(flat, AXES) / total  124 us
    psum x1, waiting for transfers between devices, on_device(): own = lax.psum(own, 'batch') / total  101 us
    pallas_call x1, Pallas kernels, solve(): pl.pallas_call(series_kernel, name='series', out_shape=outs, in_specs=[vm...  40.6 us
    reduce_scatter x1, waiting for transfers between devices, on_device(): own = lax.psum_scatter(grads, 'mp', scatter_dimension=0)  35.8 us
    all_gather x1, blocking collectives, on_device(): w_in_all = lax.all_gather(w_in, 'mp', axis=0)  13 us
    all_gather x1, blocking collectives, on_device(): w_out_all = lax.all_gather(w_out, 'mp', axis=0)  10.8 us
  transfers between devices with their start and end apart: 3, of which 3 were waited for; matrix products, arithmetic and copies ran while one was open for 1% of the time, Pallas kernels for 0%

profile of v1, /device:TPU:1, one launch (start us, length us, event | category | flops | bytes accessed | tf_op | source)
XLA Modules:
  0.0 359.6 jit_solution(17677405046736117927)
XLA Ops:
  8.0 13.0 %all-gather = bf16[1024,256]{1,0:T(8,128)(2,1)} all-gather(bf16[256,256]{1,0:T(8,128)(2,1)} %param.19), channel_id=2, replica_groups=mesh['batch'=32,'mp'=4] {'mp'}, dimensions={0}, use_global_device_ids=true | all-gather | bytes 655360 | tf_op jit(solution)/shard_map/all_gather | solution.py:276
  21.1 10.8 %all-gather.1 = bf16[1024,256]{1,0:T(8,128)(2,1)} all-gather(bf16[256,256]{1,0:T(8,128)(2,1)} %param.21), channel_id=3, replica_groups=mesh['batch'=32,'mp'=4] {'mp'}, dimensions={0}, use_global_device_ids=true | all-gather | bytes 655360 | tf_op jit(solution)/shard_map/all_gather | solution.py:277
  31.9 1.7 copy.28
  33.6 1.4 copy.25.obs_steps
  35.0 0.7 reshape.39
  35.7 6.8 %all-gather.2 = bf16[4,1,256]{2,1,0:T(2,128)(2,1)S(1)} all-gather(bf16[1,1,256]{2,1,0:T(2,128)(2,1)S(1)} %reshape.39), channel_id=1, replica_groups=mesh['batch'=32,'mp'=4] {'mp'}, dimensions={0}, use_global_device_ids=true | all-gather | bytes 2560 | tf_op jit(solution)/shard_map/all_gather | solution.py:278
  42.4 0.6 convert.1.b_in
  43.0 40.6 %series.1 = (f32[4,512,256]{2,1,0:T(8,128)}, f32[256,128]{1,0:T(8,128)}, f32[1,1024]{1,0:T(1,128)}, f32[1,256]{1,0:T(1,128)}, f32[2,128]{1,0:T(2,128)}, /*index=5*/f32[1,128]{1,0:T(1,128)}, f32[128,256]{1,0:T(8,128)}) custom-call(f32[128,256]{1,0:T(8,128)} %init.1, bf16[32,128,256]{2,1,0:T(8,128)(2,1)} %brown.1, f32[1,128]{1,0:T(1,128)} %bitcast.32, ...), custom_call_target="tpu_custom_call" | custom-call | flops 12884901888 | bytes 8388608 | tf_op jit(solution)/shard_map/series/pallas_call | solution.py:212
  83.8 0.6 copy-done.3
  84.3 0.1 reduce_sum.9
  84.5 0.1 copy-done
  84.6 0.7 pad_maximum_fusion
  85.3 0.0 all-reduce.5.cloned.1.call-start
  85.3 35.8 %reduce-scatter.2.cloned.1.call-done = f32[1,512,256]{2,1,0:T(8,128)} async-done(((f32[4,512,256]{2,1,0:T(8,128)}), f32[1,512,256]{2,1,0:T(8,128)}) %reduce-scatter.2.cloned.1.call-update) | async-done | bytes 524304 | tf_op jit(solution)/shard_map/reduce_scatter | solution.py:298
  121.2 123.6 %all-reduce.3.cloned.1.call-done = f32[34050]{0:T(1024)} async-done(((f32[34050]{0:T(1024)}), f32[34050]{0:T(1024)}) %all-reduce.3.cloned.1.call-update) | async-done | bytes 136216 | tf_op jit(solution)/shard_map/psum | solution.py:303
  244.8 0.9 broadcast_multiply_fusion.1
  245.7 0.6 slice.28
  246.3 0.5 slice.24
  246.8 0.6 dynamic_slice.3
  247.4 0.7 slice_bitcast_fusion.1
  248.1 101.4 %all-reduce.5.cloned.1.call-done = f32[512,256]{1,0:T(8,128)} async-done(((f32[512,256]{1,0:T(8,128)}), f32[512,256]{1,0:T(8,128)}) %all-reduce.5.cloned.1.call-update) | async-done | bytes 524304 | tf_op jit(solution)/shard_map/psum | solution.py:299
  349.6 1.1 broadcast_multiply_fusion
  350.6 0.7 slice_bitcast_fusion
  351.4 0.8 copy.26
  (12 shorter events, 0.2 us)
Async XLA Ops:
  8.0 113.2 %reduce-scatter.2.cloned.1.call-start = ((), (), s32[]{:S(2)}) async-start(), calls=%async_computation.2 | async-start | bytes 2621440 | tf_op jit(solution)/shard_map/reduce_scatter | solution.py:298
  83.7 0.7 copy-start.3
  83.7 0.9 copy-start
  83.7 0.9 copy-start.1
  83.7 0.9 copy-start.2
  83.7 161.1 %all-reduce.3.cloned.1.call-start = ((), (), s32[]{:S(2)}) async-start(), calls=%async_computation.1 | async-start | bytes 278528 | tf_op jit(solution)/shard_map/psum | solution.py:303
  85.3 264.3 %all-reduce.5.cloned.1.call-start = ((), (), s32[]{:S(2)}) async-start(), calls=%async_computation.3 | async-start | bytes 1048576 | tf_op jit(solution)/shard_map/psum | solution.py:299
Sparse Core Ops, SparseCore 0:
  83.8 37.2 reduce-scatter.1
Sparse Core Ops, SparseCore 1:
  89.5 155.2 all-reduce.2
  247.9 101.6 all-reduce.4

commit v2 on v1

v2 whole, which is shorter than its diff:
```python
import functools

import jax
import jax.numpy as jnp
from jax import lax
from jax.experimental import pallas as pl
from jax.experimental.pallas import tpu as pltpu
from jax.sharding import Mesh
from jax.sharding import PartitionSpec as P

F32 = jnp.float32
BF16 = jnp.bfloat16


def wide(x):
    return jnp.concatenate([x, x], axis=1)


def column(row, rows):
    return jnp.transpose(jnp.broadcast_to(row, (rows, rows)))


def series_kernel(
    init,
    brown,
    step,
    lens,
    obs_steps,
    obs,
    piece_0,
    piece_1,
    piece_2,
    piece_3,
    b_out,
    dec,
    prior,
    diff,
    place,
    keep,
    send,
    elbo,
    grad_init,
    act,
    pg,
    low,
    upd,
    scaled,
    b_in,
    w_out,
    w_in_t,
    w_out_t,
    obs_at,
    state,
    kl_acc,
    sq_acc,
    in_acc,
    out_acc,
    acc,
    acc_dec,
):
    steps, rows, width = brown.shape
    pieces = (piece_0, piece_1, piece_2, piece_3)
    parts = len(pieces)
    share = piece_0.shape[1]
    hidden = parts * share
    cols = dec.shape[1]
    seen = obs.shape[0]

    step_b = column(step[...], rows)
    root_b = jnp.sqrt(step_b)
    lens_b = column(lens[...], rows)
    inv = 1.0 / diff[...]
    for j in range(seen):
        obs_at[j] = column(obs_steps[j : j + 1, :], rows)
    for q, piece in enumerate(pieces):
        block = slice(q * share, (q + 1) * share)
        w_out[block, :] = piece[width : width + share, :]
        w_out_t[q] = jnp.transpose(piece[width : width + share, :])
        w_in_t[block, :] = jnp.transpose(piece[:width, :])
        b_in[:, block] = piece[width + share :, :].astype(F32)[:1]
    dec_t = jnp.transpose(dec[...])
    w_in_t[hidden : hidden + cols, :] = dec_t
    w_in_t[hidden + cols : hidden + 2 * cols, :] = dec_t

    state[...] = init[...]
    kl_acc[...] = jnp.zeros_like(kl_acc)
    sq_acc[...] = jnp.zeros_like(sq_acc)
    in_acc[...] = jnp.zeros_like(in_acc)
    out_acc[...] = jnp.zeros_like(out_acc)
    acc[...] = jnp.zeros_like(acc)
    acc_dec[...] = jnp.zeros_like(acc_dec)

    def observe(k, low_now):
        seen_now = jnp.dot(low_now, dec[...], preferred_element_type=F32)
        total = jnp.zeros((rows, cols), F32)
        squares = sq_acc[...]
        for j in range(seen):
            misfit = jnp.where(obs_at[j] == k, seen_now - obs[j].astype(F32), 0.0)
            squares = squares + misfit * misfit
            total = total + misfit.astype(BF16).astype(F32)
        sq_acc[...] = squares
        high = total.astype(BF16)
        pg[k, :, hidden : hidden + cols] = high
        pg[k, :, hidden + cols : hidden + 2 * cols] = (total - high.astype(F32)).astype(BF16)

    def forward(k, _):
        now = state[...]
        low_now = now.astype(BF16)
        low[k] = low_now
        for q in range(parts):
            block = slice(q * share, (q + 1) * share)
            pre = jnp.dot(low_now, pieces[q][:width, :], preferred_element_type=F32) + b_in[:, block]
            act[k, :, block] = jnp.tanh(pre).astype(BF16)
        observe(k, low_now)
        drift = (
            jnp.dot(act[k], w_out[...], preferred_element_type=F32)
            + b_out[...]
        )
        live = k < lens_b
        factor = wide(jnp.where(live, step_b, 0.0))
        noise = wide(jnp.where(live, root_b, 0.0))
        residual = (drift + prior[...] * now) * inv
        scaled[k] = residual * inv
        spent = factor * (residual * residual)
        kl_acc[...] += spent[:, :rows] + spent[:, rows:]
        state[...] = now + (factor * drift + diff[...] * noise * brown[k].astype(F32))
        return 0

    lax.fori_loop(0, steps, forward, 0)
    last = state[...].astype(BF16)
    low[steps] = last
    observe(steps, last)

    state[...] = jnp.dot(
        pg[steps, :, hidden:], w_in_t[hidden:, :], preferred_element_type=F32
    )

    def backward(i, _):
        k = steps - 1 - i
        cot = state[...]
        factor = wide(jnp.where(k < lens_b, step_b, 0.0))
        pull = scaled[k]
        update = factor * (cot + pull)
        low_up = update.astype(BF16)
        upd[k] = low_up
        out_acc[...] += jnp.sum(update.reshape(rows // 8, 8, width), axis=0)
        for q in range(parts):
            block = slice(q * share, (q + 1) * share)
            a = act[k, :, block].astype(F32)
            pre = jnp.dot(low_up, w_out_t[q], preferred_element_type=F32) * (1.0 - a * a)
            pg[k, :, block] = pre.astype(BF16)
            in_acc[:, block] += jnp.sum(pre.reshape(rows // 8, 8, share), axis=0)
        state[...] = (
            cot
            + factor * (prior[...] * pull)
            + jnp.dot(pg[k], w_in_t[...], preferred_element_type=F32)
        )
        return 0

    lax.fori_loop(0, steps, backward, 0)
    grad_init[...] = state[...]

    chunk = 4
    turned = (((0,), (0,)), ((), ()))

    def gather_grads(i, _):
        at = pl.ds(i * chunk, chunk)
        left = low[at].reshape(chunk * rows, width)
        right = pg[at].reshape(chunk * rows, hidden + 2 * cols)
        acc[0] += lax.dot_general(left, right[:, :hidden], turned, preferred_element_type=F32)
        acc_dec[...] += lax.dot_general(
            left, right[:, hidden:], turned, preferred_element_type=F32
        )
        acc[1] += lax.dot_general(
            upd[at].reshape(chunk * rows, width),
            act[at].reshape(chunk * rows, hidden),
            turned,
            preferred_element_type=F32,
        )
        return 0

    lax.fori_loop(0, steps // chunk, gather_grads, 0)
    final = acc_dec[...] + lax.dot_general(
        low[steps], pg[steps, :, hidden:], turned, preferred_element_type=F32
    )
    core = place[0]
    spot = place[1]
    slots = keep.shape[0]
    deep = width // slots
    halves = share // cols
    acc_dec[:, :cols] = final[:, :cols] + final[:, cols:]
    in_sum = jnp.sum(in_acc[...], axis=0, keepdims=True)
    out_sum = jnp.sum(out_acc[...], axis=0, keepdims=True)
    kl = 0.5 * jnp.sum(jnp.transpose(kl_acc[...]), axis=0, keepdims=True)
    loglik = -0.5 * jnp.sum(jnp.transpose(sq_acc[...]), axis=0, keepdims=True)
    rest = [out_sum[:, p * cols : (p + 1) * cols] for p in range(width // cols)]
    rest = rest + [loglik, kl]
    rest = rest + [jnp.zeros((8 - halves - len(rest), cols), F32)]
    base = halves * deep
    tile = slots * 8
    for half, out in ((core, keep), (1 - core, send)):
        decs = acc_dec[pl.ds(pl.multiple_of(half * tile, 8), tile), :cols].reshape(slots, 8, cols)
        for s in range(parts):
            q = lax.rem(spot + (parts - s), parts)
            aux = [in_sum[:, s * share + p * cols : s * share + (p + 1) * cols] for p in range(halves)]
            aux = jnp.concatenate(aux + rest, axis=0)
            for p in range(halves):
                block = slice(s * share + p * cols, s * share + (p + 1) * cols)
                out[:, q, p * deep : (p + 1) * deep, :] = acc[half, :, block].reshape(
                    slots, deep, cols
                )
            out[:, q, base : base + 8, :] = decs
            out[:, q, base + 8 : base + 16, :] = jnp.broadcast_to(aux[None], (slots, 8, cols))
    divisor = (width * lens[...] + cols * seen).astype(F32)
    elbo[...] = (loglik - kl) / divisor


def solve(init, brown, step, lengths, obs_steps, observed, pieces, b_out, dec, prior, diff, place, slots):
    rows, width = init.shape
    steps = brown.shape[0]
    parts = len(pieces)
    share = pieces[0].shape[1]
    hidden = parts * share
    seen, cols = observed.shape[1:]
    vmem = pl.BlockSpec(memory_space=pltpu.VMEM)
    shape = jax.ShapeDtypeStruct
    payload = shape((slots, parts, width // slots * share // cols + 16, cols), F32)
    outs = (
        payload,
        payload,
        shape((1, rows), F32),
        shape((rows, width), F32),
    )
    return pl.pallas_call(
        series_kernel,
        name="series",
        out_shape=outs,
        in_specs=[vmem] * (10 + parts) + [pl.BlockSpec(memory_space=pltpu.SMEM)],
        out_specs=(vmem,) * len(outs),
        scratch_shapes=[
            pltpu.VMEM((steps, rows, hidden), BF16),
            pltpu.VMEM((steps + 1, rows, hidden + 2 * cols), BF16),
            pltpu.VMEM((steps + 1, rows, width), BF16),
            pltpu.VMEM((steps, rows, width), BF16),
            pltpu.VMEM((steps, rows, width), F32),
            pltpu.VMEM((1, hidden), F32),
            pltpu.VMEM((hidden, width), BF16),
            pltpu.VMEM((hidden + 2 * cols, width), BF16),
            pltpu.VMEM((parts, width, share), BF16),
            pltpu.VMEM((seen, rows, cols), jnp.int32),
            pltpu.VMEM((rows, width), F32),
            pltpu.VMEM((rows, rows), F32),
            pltpu.VMEM((rows, cols), F32),
            pltpu.VMEM((8, hidden), F32),
            pltpu.VMEM((8, width), F32),
            pltpu.VMEM((2, width, hidden), F32),
            pltpu.VMEM((width, 2 * cols), F32),
        ],
        compiler_params=pltpu.CompilerParams(vmem_limit_bytes=48 * 1024 * 1024),
        cost_estimate=pl.CostEstimate(
            flops=12 * steps * rows * width * hidden,
            bytes_accessed=8 * 1024 * 1024,
            transcendentals=steps * rows * hidden,
        ),
    )(
        init,
        brown,
        step[None],
        lengths[None],
        obs_steps.T,
        jnp.transpose(observed, (1, 0, 2)),
        *pieces,
        b_out[None],
        dec,
        prior[None],
        diff[None],
        place,
    )


def sum_kernel(scale, parts, spread, rest):
    depth = spread.shape[1]
    total = jnp.sum(parts[...], axis=0) * scale
    spread[...] = jnp.broadcast_to(total[None, :depth], spread.shape)
    rest[...] = total[depth:]


def sum_parts(parts, slots, scale):
    _, depth, cols = parts.shape
    vmem = pl.BlockSpec(memory_space=pltpu.VMEM)
    return pl.pallas_call(
        functools.partial(sum_kernel, scale),
        name="sum_parts",
        out_shape=(
            jax.ShapeDtypeStruct((slots, depth - 8, cols), F32),
            jax.ShapeDtypeStruct((8, cols), F32),
        ),
        in_specs=[vmem],
        out_specs=(vmem, vmem),
        compiler_params=pltpu.CompilerParams(vmem_limit_bytes=8 * 1024 * 1024),
    )(parts)


def lay_kernel(place, mine, other, w_in, w_out, dec):
    core = place[0]
    slots, depth, cols = mine.shape
    width = w_in.shape[0]
    deep = width // slots

    def lay(low, high):
        for p in range(w_in.shape[1] // cols):
            rows = slice(p * deep, (p + 1) * deep)
            block = slice(p * cols, (p + 1) * cols)
            w_in[:, block] = low[:, rows, :].reshape(width, cols)
            w_out[block, :] = jnp.transpose(high[:, rows, :].reshape(width, cols))
        dec[: slots * 8, :] = low[:, depth - 8 :, :].reshape(slots * 8, cols)
        dec[slots * 8 :, :] = high[:, depth - 8 :, :].reshape(slots * 8, cols)

    pl.when(core == 0)(lambda: lay(mine, other))
    pl.when(core == 1)(lambda: lay(other, mine))


def lay_out(place, mine, other, width, share, cols):
    vmem = pl.BlockSpec(memory_space=pltpu.VMEM)
    shape = jax.ShapeDtypeStruct
    return pl.pallas_call(
        lay_kernel,
        name="lay_out",
        out_shape=(
            shape((width, share), F32),
            shape((share, width), F32),
            shape((width, cols), F32),
        ),
        in_specs=[pl.BlockSpec(memory_space=pltpu.SMEM), vmem, vmem],
        out_specs=(vmem,) * 3,
        compiler_params=pltpu.CompilerParams(vmem_limit_bytes=8 * 1024 * 1024),
    )(place, mine, other)


AXES = ("y", "z", "c", "x")
RING = ("y", "z", "x")


def shifted(array, axis, by):
    count = lax.axis_size(axis)
    return lax.ppermute(array, axis, [(i, (i + by) % count) for i in range(count)])


def on_device(
    init_state,
    brownian,
    step_size,
    lengths,
    obs_steps,
    observed,
    w_in,
    b_in,
    w_out,
    b_out,
    decoder,
    prior_rate,
    diffusion,
):
    width = init_state.shape[1]
    share = w_in.shape[1]
    parts = lax.axis_size("x")
    slots = lax.axis_size("y") * lax.axis_size("z")
    cols = decoder.shape[1]
    core = lax.axis_index("c")
    spot = lax.axis_index("x")

    mine = jnp.concatenate([w_in, w_out, jnp.broadcast_to(b_in[None], (16, share))], axis=0)
    pieces = [mine] + [shifted(mine, "x", by) for by in range(1, parts)]
    place = jnp.stack([core, spot]).astype(jnp.int32)
    keep, send, elbo, grad_init = solve(
        init_state,
        brownian,
        step_size,
        lengths,
        obs_steps,
        observed,
        pieces,
        b_out,
        decoder,
        prior_rate,
        diffusion,
        place,
        slots,
    )
    scale = 1.0 / (init_state.shape[0] * lax.axis_size(AXES))
    chip = keep + shifted(send, "c", 1)
    members = slots * parts
    received = lax.all_to_all(chip.reshape(members, -1, cols), RING, 0, 0, tiled=True)
    spread, rest = sum_parts(received, slots, scale)
    own = lax.all_to_all(spread, ("y", "z"), 0, 0, tiled=True)
    other = shifted(own, "c", 1)
    grad_w_in, grad_w_out, grad_decoder = lay_out(place, own, other, width, share, cols)
    per = share // cols
    end = per + width // cols
    return (
        elbo.reshape(-1),
        jnp.sum(rest[end : end + 2], axis=1),
        grad_w_in,
        rest[:per].reshape(-1),
        grad_w_out,
        rest[per:end].reshape(-1),
        grad_decoder,
        grad_init,
    )


def solution(mesh):
    torus = Mesh(mesh.devices.reshape(4, 4, 2, mesh.shape["mp"]), AXES)
    return jax.shard_map(
        on_device,
        mesh=torus,
        in_specs=(
            P(AXES, None),
            P(None, AXES, None),
            P(AXES),
            P(AXES),
            P(AXES, None),
            P(AXES, None, None),
            P(None, "x"),
            P("x"),
            P("x", None),
            P(),
            P(),
            P(),
            P(),
        ),
        out_specs=(
            P(AXES),
            P(),
            P(None, "x"),
            P("x"),
            P("x", None),
            P(),
            P(),
            P(AXES, None),
        ),
        check_vma=False,
    )
```

time: 360 us -> 120 us (0.33)
  waiting for transfers between devices: 261 us -> 16.6 us
  between operations: 15.5 us -> 0.66 us
  blocking collectives: 30.6 us -> 42.7 us
  starting transfers between devices: 0.13 us -> 8.09 us
    psum x2 -> x0, waiting for transfers between devices: 225 us -> none  [the longest x1 124 us: on_device(): flat = lax.psum(flat, AXES) / total]
    all_to_all x0 -> x2, blocking collectives: none -> 42.7 us  [the longest x1 32.4 us: on_device(): lax.all_to_all(chip.reshape(members, -1, cols), RING, 0, 0, tiled=True)]
    reduce_scatter x1 -> x0, waiting for transfers between devices: 35.8 us -> none  [on_device(): own = lax.psum_scatter(grads, 'mp', scatter_dimension=0)]
    all_gather x3 -> x0, blocking collectives: 30.6 us -> none  [the longest x1 13 us: on_device(): w_in_all = lax.all_gather(w_in, 'mp', axis=0)]
    ppermute x0 -> x5, waiting for transfers between devices: none -> 16.6 us  [shifted(): lax.ppermute(array, axis, [(i, (i + by) % count) for i in range(count)])]
    ppermute x0 -> x5, starting transfers between devices: none -> 8.09 us  [shifted(): lax.ppermute(array, axis, [(i, (i + by) % count) for i in range(count)])]
  transfers between devices with their start and end apart: 3 -> 5, of which waited for: 3 -> 5; matrix products, arithmetic and copies ran while one was open for 1% -> 2% of each run, Pallas kernels for 0% -> 0%
where the time goes in v2:
time: 120 us; the launch traced here: 119 us
  blocking collectives  42.7 us (36%)
  Pallas kernels  41.5 us (35%)
  waiting for transfers between devices  16.6 us (14%)
  starting transfers between devices  8.09 us (7%)
  local copies, waits for them, and re-layouts  7.42 us (6%)
  other arithmetic  2.44 us (2%)
    pallas_call x1, Pallas kernels, solve(): pl.pallas_call(series_kernel, name='series', out_shape=outs, in_specs=[vm...  39.9 us
    all_to_all x1, blocking collectives, on_device(): lax.all_to_all(chip.reshape(members, -1, cols), RING, 0, 0, tiled=True)  32.4 us
    ppermute x5, waiting for transfers between devices, shifted(): lax.ppermute(array, axis, [(i, (i + by) % count) for i in range(count)])  16.6 us
    all_to_all x1, blocking collectives, on_device(): own = lax.all_to_all(spread, ('y', 'z'), 0, 0, tiled=True)  10.3 us
    ppermute x5, starting transfers between devices, shifted(): lax.ppermute(array, axis, [(i, (i + by) % count) for i in range(count)])  8.09 us
    unnamed x17, local copies, waits for them, and re-layouts  6.76 us
  transfers between devices with their start and end apart: 5, of which 5 were waited for; matrix products, arithmetic and copies ran while one was open for 2% of the time, Pallas kernels for 0%

profile of v2, /device:TPU:1, one launch (start us, length us, event | category | flops | bytes accessed | tf_op | source)
XLA Modules:
  0.0 119.4 jit_solution(5014993475958651706)
XLA Ops:
  0.6 0.7 broadcast_in_dim.23
  1.3 1.0 pad_maximum_fusion.piece_0
  2.3 3.4 %collective-permute-start.2 = (bf16[528,256]{1,0:T(8,128)(2,1)S(1)}, bf16[528,256]{1,0:T(8,128)(2,1)S(1)}, u32[]{:S(2)}, u32[]{:S(2)}) collective-permute-start(bf16[528,256]{1,0:T(8,128)(2,1)S(1)} %pad_maximum_fusion.piece_0), channel_id=1, source_target_pairs={{0,3},{1,0},{2,1},{3,2},{4,7},{5,4},{6,5},{7,6},{8,11},{9,8},{10,9... | collective-permute-start | bytes 811016 | tf_op jit(solution)/shard_map/ppermute | solution.py:346
  5.6 0.5 collective-permute-start.1
  6.2 0.6 collective-permute-start
  6.8 1.0 copy.23
  7.8 4.1 %collective-permute-done.2.piece_3 = bf16[528,256]{1,0:T(8,128)(2,1)S(1)} collective-permute-done((bf16[528,256]{1,0:T(8,128)(2,1)S(1)}, bf16[528,256]{1,0:T(8,128)(2,1)S(1)}, u32[]{:S(2)}, u32[]{:S(2)}) %collective-permute-start.2) | collective-permute-done | bytes 270368 | tf_op jit(solution)/shard_map/ppermute | solution.py:346
  11.9 2.3 %collective-permute-done.1.piece_2 = bf16[528,256]{1,0:T(8,128)(2,1)S(1)} collective-permute-done((bf16[528,256]{1,0:T(8,128)(2,1)S(1)}, bf16[528,256]{1,0:T(8,128)(2,1)S(1)}, u32[]{:S(2)}, u32[]{:S(2)}) %collective-permute-start.1) | collective-permute-done | bytes 270368 | tf_op jit(solution)/shard_map/ppermute | solution.py:346
  14.3 7.1 %collective-permute-done.piece_1 = bf16[528,256]{1,0:T(8,128)(2,1)S(1)} collective-permute-done((bf16[528,256]{1,0:T(8,128)(2,1)S(1)}, bf16[528,256]{1,0:T(8,128)(2,1)S(1)}, u32[]{:S(2)}, u32[]{:S(2)}) %collective-permute-start) | collective-permute-done | bytes 270368 | tf_op jit(solution)/shard_map/ppermute | solution.py:346
  21.4 0.9 copy-done
  22.3 0.8 copy-done.1
  23.1 0.7 copy-done.2
  23.8 0.7 copy-done.3
  24.5 0.7 copy-done.4
  25.1 0.7 copy-done.5
  25.8 0.7 copy-done.6
  26.5 0.7 copy-done.7
  27.1 39.9 %series.1 = (f32[16,4,48,128]{3,2,1,0:T(8,128)S(1)}, f32[16,4,48,128]{3,2,1,0:T(8,128)S(1)}, f32[1,128]{1,0:T(1,128)}, f32[128,256]{1,0:T(8,128)}) custom-call(f32[128,256]{1,0:T(8,128)S(1)} %copy-done, bf16[32,128,256]{2,1,0:T(8,128)(2,1)} %brown.1, f32[1,128]{1,0:T(1,128)S(1)} %bitcast.22, s32[1,128]{1,0:T(1,128)S(1)} %bitcast.23, s32[8,128]{1,0:T(8,128)S(1)} %bitcast.18, ...), custom_call_target="tpu_custom_call" | custom-call | flops 12884901888 | bytes 8388608 | tf_op jit(solution)/shard_map/series/pallas_call | solution.py:234
  67.5 3.0 %collective-permute-done.3 = f32[16,4,48,128]{3,2,1,0:T(8,128)S(1)} collective-permute-done((f32[16,4,48,128]{3,2,1,0:T(8,128)S(1)}, f32[16,4,48,128]{3,2,1,0:T(8,128)S(1)}, u32[]{:S(2)}, u32[]{:S(2)}) %collective-permute-start.3) | collective-permute-done | bytes 1572896 | tf_op jit(solution)/shard_map/ppermute | solution.py:346
  70.8 32.4 %all_to_all.10.parts = f32[64,48,128]{2,1,0:T(8,128)S(1)} all-to-all(f32[64,48,128]{2,1,0:T(8,128)S(1)} %bitcast.24), channel_id=1, replica_groups=mesh['y'=4,'z'=4,'c'=2,'x'=4] {'y','z','x'}, dimensions={0} | all-to-all | bytes 3145728 | tf_op jit(solution)/shard_map/all_to_all | solution.py:393
  103.3 10.3 %all_to_all.11.mine = f32[16,40,128]{2,1,0:T(8,128)S(1)} all-to-all(f32[16,40,128]{2,1,0:T(8,128)S(1)} %get-tuple-element.21), channel_id=1, replica_groups=mesh['y'=4,'z'=4,'c'=2,'x'=4] {'y','z'}, dimensions={0} | all-to-all | bytes 655360 | tf_op jit(solution)/shard_map/all_to_all | solution.py:395
  113.6 3.1 %collective-permute-start.4 = (f32[16,40,128]{2,1,0:T(8,128)S(1)}, f32[16,40,128]{2,1,0:T(8,128)S(1)}, u32[]{:S(2)}, u32[]{:S(2)}) collective-permute-start(f32[16,40,128]{2,1,0:T(8,128)S(1)} %all_to_all.11.mine), channel_id=1, source_target_pairs={{0,4},{4,0},{1,5},{5,1},{2,6},{6,2},{3,7},{7,3},{8,12},{12,8},{9,1... | collective-permute-start | bytes 983048 | tf_op jit(solution)/shard_map/ppermute | solution.py:346
  116.7 1.2 slice_bitcast_fusion
  117.9 1.5 %lay_out.1 = (f32[256,256]{1,0:T(8,128)}, f32[256,256]{1,0:T(8,128)}, f32[256,128]{1,0:T(8,128)}) custom-call(s32[2]{0:T(128)S(1)} %pad_add_fusion.place, f32[16,40,128]{2,1,0:T(8,128)S(1)} %all_to_all.11.mine, f32[16,40,128]{2,1,0:T(8,128)S(1)} %collective-permute-done.4.other), custom_call_target="tpu_custom_call" | custom-call | tf_op jit(solution)/shard_map/lay_out/pallas_call | solution.py:326
  (13 shorter events, 1.0 us)
Async XLA Ops:
  2.3 9.7 %collective-permute-start.2 = (bf16[528,256]{1,0:T(8,128)(2,1)S(1)}, bf16[528,256]{1,0:T(8,128)(2,1)S(1)}, u32[]{:S(2)}, u32[]{:S(2)}) collective-permute-start(bf16[528,256]{1,0:T(8,128)(2,1)S(1)} %pad_maximum_fusion.piece_0), channel_id=1, source_target_pairs={{0,3},{1,0},{2,1},{3,2},{4,7},{5,4},{6,5},{7,6},{8,11},{9,8},{10,9... | collective-permute-start | bytes 811016 | tf_op jit(solution)/shard_map/ppermute | solution.py:346
  5.6 8.6 %collective-permute-start.1 = (bf16[528,256]{1,0:T(8,128)(2,1)S(1)}, bf16[528,256]{1,0:T(8,128)(2,1)S(1)}, u32[]{:S(2)}, u32[]{:S(2)}) collective-permute-start(bf16[528,256]{1,0:T(8,128)(2,1)S(1)} %pad_maximum_fusion.piece_0), channel_id=1, source_target_pairs={{0,2},{1,3},{2,0},{3,1},{4,6},{5,7},{6,4},{7,5},{8,10},{9,11},{10,... | collective-permute-start | bytes 811016 | tf_op jit(solution)/shard_map/ppermute | solution.py:346
  6.2 15.2 %collective-permute-start = (bf16[528,256]{1,0:T(8,128)(2,1)S(1)}, bf16[528,256]{1,0:T(8,128)(2,1)S(1)}, u32[]{:S(2)}, u32[]{:S(2)}) collective-permute-start(bf16[528,256]{1,0:T(8,128)(2,1)S(1)} %pad_maximum_fusion.piece_0), channel_id=1, source_target_pairs={{0,1},{1,2},{2,3},{3,0},{4,5},{5,6},{6,7},{7,4},{8,9},{9,10},{10,1... | collective-permute-start | bytes 811016 | tf_op jit(solution)/shard_map/ppermute | solution.py:346
  21.3 0.9 copy-start
  22.3 0.8 copy-start.1
  23.1 0.7 copy-start.2
  23.8 0.7 copy-start.3
  24.5 0.7 copy-start.4
  25.1 0.7 copy-start.5
  25.8 0.7 copy-start.6
  26.5 0.7 copy-start.7
  67.0 3.5 %collective-permute-start.3 = (f32[16,4,48,128]{3,2,1,0:T(8,128)S(1)}, f32[16,4,48,128]{3,2,1,0:T(8,128)S(1)}, u32[]{:S(2)}, u32[]{:S(2)}) collective-permute-start(f32[16,4,48,128]{3,2,1,0:T(8,128)S(1)} %get-tuple-element.19), channel_id=1, source_target_pairs={{0,4},{4,0},{1,5},{5,1},{2,6},{6,2},{3,7},{7,3},{8,12},{12,8},{9,1... | collective-permute-start | bytes 4718600 | tf_op jit(solution)/shard_map/ppermute | solution.py:346
  113.6 4.4 %collective-permute-start.4 = (f32[16,40,128]{2,1,0:T(8,128)S(1)}, f32[16,40,128]{2,1,0:T(8,128)S(1)}, u32[]{:S(2)}, u32[]{:S(2)}) collective-permute-start(f32[16,40,128]{2,1,0:T(8,128)S(1)} %all_to_all.11.mine), channel_id=1, source_target_pairs={{0,4},{4,0},{1,5},{5,1},{2,6},{6,2},{3,7},{7,3},{8,12},{12,8},{9,1... | collective-permute-start | bytes 983048 | tf_op jit(solution)/shard_map/ppermute | solution.py:346

commit v3 on v2

--- a/solution.py
+++ b/solution.py
@@ -21,29 +21,25 @@
 
 
 def series_kernel(
-    init,
-    brown,
-    step,
-    lens,
-    obs_steps,
+    brown_home,
+    packed,
     obs,
     piece_0,
     piece_1,
     piece_2,
     piece_3,
-    b_out,
-    dec,
-    prior,
-    diff,
     place,
     keep,
     send,
     elbo,
     grad_init,
     act,
-    pg,
+    seen_back,
     low,
-    upd,
+    pg_a,
+    pg_b,
+    upd_a,
+    upd_b,
     scaled,
     b_in,
     w_out,
@@ -57,7 +53,12 @@
     out_acc,
     acc,
     acc_dec,
+    brown,
+    dec,
+    done,
 ):
+    fetch = pltpu.make_async_copy(brown_home, brown, done)
+    fetch.start()
     steps, rows, width = brown.shape
     pieces = (piece_0, piece_1, piece_2, piece_3)
     parts = len(pieces)
@@ -65,24 +66,31 @@
     hidden = parts * share
     cols = dec.shape[1]
     seen = obs.shape[0]
-
-    step_b = column(step[...], rows)
-    root_b = jnp.sqrt(step_b)
-    lens_b = column(lens[...], rows)
-    inv = 1.0 / diff[...]
-    for j in range(seen):
-        obs_at[j] = column(obs_steps[j : j + 1, :], rows)
+    first, last_row = packed[:rows, :], packed[rows : rows + 8, :]
+    b_out, prior, diff = last_row[0:1], last_row[1:2], last_row[2:3]
+    step, lens = last_row[3:4, :rows], last_row[3:4, rows:]
+    dec_home = packed[rows + 8 :, :].astype(BF16)
+    dec[:rows, :] = dec_home[:, :cols]
+    dec[rows:, :] = dec_home[:, cols:]
+
     for q, piece in enumerate(pieces):
         block = slice(q * share, (q + 1) * share)
         w_out[block, :] = piece[width : width + share, :]
         w_out_t[q] = jnp.transpose(piece[width : width + share, :])
         w_in_t[block, :] = jnp.transpose(piece[:width, :])
         b_in[:, block] = piece[width + share :, :].astype(F32)[:1]
+    step_b = column(step, rows)
+    root_b = jnp.sqrt(step_b)
+    lens_b = column(lens, rows)
+    inv = 1.0 / diff
+    for j in range(seen):
+        half = (j % 2) * rows
+        obs_at[j] = column(last_row[4 + j // 2 : 5 + j // 2, half : half + rows], rows)
     dec_t = jnp.transpose(dec[...])
     w_in_t[hidden : hidden + cols, :] = dec_t
     w_in_t[hidden + cols : hidden + 2 * cols, :] = dec_t
 
-    state[...] = init[...]
+    state[...] = first
     kl_acc[...] = jnp.zeros_like(kl_acc)
     sq_acc[...] = jnp.zeros_like(sq_acc)
     in_acc[...] = jnp.zeros_like(in_acc)
@@ -91,17 +99,18 @@
     acc_dec[...] = jnp.zeros_like(acc_dec)
 
     def observe(k, low_now):
+        k_now = jnp.asarray(k, jnp.int32).astype(F32)
         seen_now = jnp.dot(low_now, dec[...], preferred_element_type=F32)
         total = jnp.zeros((rows, cols), F32)
         squares = sq_acc[...]
         for j in range(seen):
-            misfit = jnp.where(obs_at[j] == k, seen_now - obs[j].astype(F32), 0.0)
+            misfit = jnp.where(obs_at[j] == k_now, seen_now - obs[j].astype(F32), 0.0)
             squares = squares + misfit * misfit
             total = total + misfit.astype(BF16).astype(F32)
         sq_acc[...] = squares
         high = total.astype(BF16)
-        pg[k, :, hidden : hidden + cols] = high
-        pg[k, :, hidden + cols : hidden + 2 * cols] = (total - high.astype(F32)).astype(BF16)
+        seen_back[k, :, :cols] = high
+        seen_back[k, :, cols:] = (total - high.astype(F32)).astype(BF16)
 
     def forward(k, _):
         now = state[...]
@@ -114,74 +123,84 @@
         observe(k, low_now)
         drift = (
             jnp.dot(act[k], w_out[...], preferred_element_type=F32)
-            + b_out[...]
+            + b_out
         )
-        live = k < lens_b
+        live = k.astype(F32) < lens_b
         factor = wide(jnp.where(live, step_b, 0.0))
         noise = wide(jnp.where(live, root_b, 0.0))
-        residual = (drift + prior[...] * now) * inv
+        residual = (drift + prior * now) * inv
         scaled[k] = residual * inv
         spent = factor * (residual * residual)
         kl_acc[...] += spent[:, :rows] + spent[:, rows:]
-        state[...] = now + (factor * drift + diff[...] * noise * brown[k].astype(F32))
+        state[...] = now + (factor * drift + diff * noise * brown[k].astype(F32))
         return 0
 
+    fetch.wait()
     lax.fori_loop(0, steps, forward, 0)
     last = state[...].astype(BF16)
     low[steps] = last
     observe(steps, last)
 
     state[...] = jnp.dot(
-        pg[steps, :, hidden:], w_in_t[hidden:, :], preferred_element_type=F32
-    )
-
-    def backward(i, _):
-        k = steps - 1 - i
-        cot = state[...]
-        factor = wide(jnp.where(k < lens_b, step_b, 0.0))
-        pull = scaled[k]
-        update = factor * (cot + pull)
-        low_up = update.astype(BF16)
-        upd[k] = low_up
-        out_acc[...] += jnp.sum(update.reshape(rows // 8, 8, width), axis=0)
-        for q in range(parts):
-            block = slice(q * share, (q + 1) * share)
-            a = act[k, :, block].astype(F32)
-            pre = jnp.dot(low_up, w_out_t[q], preferred_element_type=F32) * (1.0 - a * a)
-            pg[k, :, block] = pre.astype(BF16)
-            in_acc[:, block] += jnp.sum(pre.reshape(rows // 8, 8, share), axis=0)
-        state[...] = (
-            cot
-            + factor * (prior[...] * pull)
-            + jnp.dot(pg[k], w_in_t[...], preferred_element_type=F32)
-        )
-        return 0
-
-    lax.fori_loop(0, steps, backward, 0)
-    grad_init[...] = state[...]
-
-    chunk = 4
+        seen_back[steps], w_in_t[hidden:, :], preferred_element_type=F32
+    )
+
     turned = (((0,), (0,)), ((), ()))
 
-    def gather_grads(i, _):
-        at = pl.ds(i * chunk, chunk)
-        left = low[at].reshape(chunk * rows, width)
-        right = pg[at].reshape(chunk * rows, hidden + 2 * cols)
+    def back_pair(k_low, pg_now, upd_now):
+        for slot in (1, 0):
+            k = k_low + slot
+            cot = state[...]
+            factor = wide(jnp.where(k.astype(F32) < lens_b, step_b, 0.0))
+            pull = scaled[k]
+            update = factor * (cot + pull)
+            low_up = update.astype(BF16)
+            upd_now[slot] = low_up
+            out_acc[...] += jnp.sum(update.reshape(rows // 8, 8, width), axis=0)
+            for q in range(parts):
+                block = slice(q * share, (q + 1) * share)
+                a = act[k, :, block].astype(F32)
+                pre = jnp.dot(low_up, w_out_t[q], preferred_element_type=F32) * (1.0 - a * a)
+                pg_now[slot, :, block] = pre.astype(BF16)
+                in_acc[:, block] += jnp.sum(pre.reshape(rows // 8, 8, share), axis=0)
+            pg_now[slot, :, hidden:] = seen_back[k]
+            state[...] = (
+                cot
+                + factor * (prior * pull)
+                + jnp.dot(pg_now[slot], w_in_t[...], preferred_element_type=F32)
+            )
+
+    def add_grads(k_low, pg_then, upd_then):
+        at = pl.ds(k_low, 2)
+        left = low[at].reshape(2 * rows, width)
+        right = pg_then[...].reshape(2 * rows, hidden + 2 * cols)
         acc[0] += lax.dot_general(left, right[:, :hidden], turned, preferred_element_type=F32)
         acc_dec[...] += lax.dot_general(
             left, right[:, hidden:], turned, preferred_element_type=F32
         )
         acc[1] += lax.dot_general(
-            upd[at].reshape(chunk * rows, width),
-            act[at].reshape(chunk * rows, hidden),
+            upd_then[...].reshape(2 * rows, width),
+            act[at].reshape(2 * rows, hidden),
             turned,
             preferred_element_type=F32,
         )
+
+    pg_b[...] = jnp.zeros_like(pg_b)
+    upd_b[...] = jnp.zeros_like(upd_b)
+
+    def backward(i, _):
+        k = steps - 4 - 4 * i
+        back_pair(k + 2, pg_a, upd_a)
+        add_grads(jnp.minimum(k + 4, steps - 2), pg_b, upd_b)
+        back_pair(k, pg_b, upd_b)
+        add_grads(k + 2, pg_a, upd_a)
         return 0
 
-    lax.fori_loop(0, steps // chunk, gather_grads, 0)
+    lax.fori_loop(0, steps // 4, backward, 0)
+    add_grads(0, pg_b, upd_b)
+    grad_init[...] = state[...]
     final = acc_dec[...] + lax.dot_general(
-        low[steps], pg[steps, :, hidden:], turned, preferred_element_type=F32
+        low[steps], seen_back[steps], turned, preferred_element_type=F32
     )
     core = place[0]
     spot = place[1]
@@ -211,7 +230,7 @@
                 )
             out[:, q, base : base + 8, :] = decs
             out[:, q, base + 8 : base + 16, :] = jnp.broadcast_to(aux[None], (slots, 8, cols))
-    divisor = (width * lens[...] + cols * seen).astype(F32)
+    divisor = width * lens + cols * seen
     elbo[...] = (loglik - kl) / divisor
 
 
@@ -223,7 +242,21 @@
     hidden = parts * share
     seen, cols = observed.shape[1:]
     vmem = pl.BlockSpec(memory_space=pltpu.VMEM)
+    home = pl.BlockSpec(memory_space=pltpu.HBM)
     shape = jax.ShapeDtypeStruct
+    ends = jnp.concatenate([step, lengths.astype(F32)])[None]
+    packed = jnp.concatenate(
+        [
+            init,
+            b_out[None],
+            prior[None],
+            diff[None],
+            ends,
+            obs_steps.T.astype(F32).reshape(seen // 2, 2 * rows),
+            jnp.concatenate([dec[:rows], dec[rows:]], axis=1).astype(F32),
+        ],
+        axis=0,
+    )
     payload = shape((slots, parts, width // slots * share // cols + 16, cols), F32)
     outs = (
         payload,
@@ -235,19 +268,24 @@
         series_kernel,
         name="series",
         out_shape=outs,
-        in_specs=[vmem] * (10 + parts) + [pl.BlockSpec(memory_space=pltpu.SMEM)],
+        in_specs=[home]
+        + [vmem] * (2 + parts)
+        + [pl.BlockSpec(memory_space=pltpu.SMEM)],
         out_specs=(vmem,) * len(outs),
         scratch_shapes=[
             pltpu.VMEM((steps, rows, hidden), BF16),
-            pltpu.VMEM((steps + 1, rows, hidden + 2 * cols), BF16),
+            pltpu.VMEM((steps + 1, rows, 2 * cols), BF16),
             pltpu.VMEM((steps + 1, rows, width), BF16),
-            pltpu.VMEM((steps, rows, width), BF16),
+            pltpu.VMEM((2, rows, hidden + 2 * cols), BF16),
+            pltpu.VMEM((2, rows, hidden + 2 * cols), BF16),
+            pltpu.VMEM((2, rows, width), BF16),
+            pltpu.VMEM((2, rows, width), BF16),
             pltpu.VMEM((steps, rows, width), F32),
             pltpu.VMEM((1, hidden), F32),
             pltpu.VMEM((hidden, width), BF16),
             pltpu.VMEM((hidden + 2 * cols, width), BF16),
             pltpu.VMEM((parts, width, share), BF16),
-            pltpu.VMEM((seen, rows, cols), jnp.int32),
+            pltpu.VMEM((seen, rows, cols), F32),
             pltpu.VMEM((rows, width), F32),
             pltpu.VMEM((rows, rows), F32),
             pltpu.VMEM((rows, cols), F32),
@@ -255,6 +293,9 @@
             pltpu.VMEM((8, width), F32),
             pltpu.VMEM((2, width, hidden), F32),
             pltpu.VMEM((width, 2 * cols), F32),
+            pltpu.VMEM((steps, rows, width), BF16),
+            pltpu.VMEM((width, cols), BF16),
+            pltpu.SemaphoreType.DMA,
         ],
         compiler_params=pltpu.CompilerParams(vmem_limit_bytes=48 * 1024 * 1024),
         cost_estimate=pl.CostEstimate(
@@ -263,26 +304,58 @@
             transcendentals=steps * rows * hidden,
         ),
     )(
-        init,
         brown,
-        step[None],
-        lengths[None],
-        obs_steps.T,
+        packed,
         jnp.transpose(observed, (1, 0, 2)),
         *pieces,
-        b_out[None],
-        dec,
-        prior[None],
-        diff[None],
         place,
     )
+
+
+def encode_kernel(mine, other, coded):
+    total = mine[...] + other[...]
+    depth = total.shape[1] - 16
+
+    def scaled_part(part):
+        peak = jnp.max(jnp.abs(part), axis=1, keepdims=True)
+        power = jnp.floor(jnp.log2(jnp.maximum(peak, 1e-30))) + 1.0
+        return part * jnp.exp2(14.0 - power), power
+
+    weights, weights_power = scaled_part(total[:, :depth])
+    decs, decs_power = scaled_part(total[:, depth : depth + 8])
+    rest, rest_power = scaled_part(total[:, depth + 8 :])
+    rest_high = jnp.round(rest)
+    rest_low = (rest - rest_high) * 16384.0
+    row = lax.broadcasted_iota(jnp.int32, rest.shape, 1)
+    powers = jnp.where(row == 0, weights_power, jnp.where(row == 1, decs_power, rest_power))
+    full = jnp.concatenate([weights, decs, rest_high, rest_low, powers], axis=1)
+    coded[...] = jnp.round(full).astype(jnp.int32).astype(jnp.int16)
+
+
+def encode(mine, other):
+    members, depth, cols = mine.shape
+    vmem = pl.BlockSpec(memory_space=pltpu.VMEM)
+    return pl.pallas_call(
+        encode_kernel,
+        name="encode",
+        out_shape=jax.ShapeDtypeStruct((members, depth + 16, cols), jnp.int16),
+        in_specs=[vmem, vmem],
+        out_specs=vmem,
+        compiler_params=pltpu.CompilerParams(vmem_limit_bytes=16 * 1024 * 1024),
+    )(mine, other)
 
 
 def sum_kernel(scale, parts, spread, rest):
     depth = spread.shape[1]
-    total = jnp.sum(parts[...], axis=0) * scale
-    spread[...] = jnp.broadcast_to(total[None, :depth], spread.shape)
-    rest[...] = total[depth:]
+    weights = depth - 8
+    values = parts[...].astype(jnp.int32).astype(F32)
+    units = jnp.exp2(values[:, depth + 16 :] - 14.0) * scale
+    main = jnp.sum(values[:, :weights] * units[:, 0:1], axis=0)
+    decs = jnp.sum(values[:, weights:depth] * units[:, 1:2], axis=0)
+    high, low = values[:, depth : depth + 8], values[:, depth + 8 : depth + 16]
+    rest[...] = jnp.sum((high + low * (1.0 / 16384.0)) * units[:, 2:3], axis=0)
+    spread[:, :weights] = jnp.broadcast_to(main[None], (spread.shape[0], *main.shape))
+    spread[:, weights:] = jnp.broadcast_to(decs[None], (spread.shape[0], *decs.shape))
 
 
 def sum_parts(parts, slots, scale):
@@ -292,12 +365,12 @@
         functools.partial(sum_kernel, scale),
         name="sum_parts",
         out_shape=(
-            jax.ShapeDtypeStruct((slots, depth - 8, cols), F32),
+            jax.ShapeDtypeStruct((slots, depth - 24, cols), F32),
             jax.ShapeDtypeStruct((8, cols), F32),
         ),
         in_specs=[vmem],
         out_specs=(vmem, vmem),
-        compiler_params=pltpu.CompilerParams(vmem_limit_bytes=8 * 1024 * 1024),
+        compiler_params=pltpu.CompilerParams(vmem_limit_bytes=16 * 1024 * 1024),
     )(parts)
 
 
@@ -388,9 +461,10 @@
         slots,
     )
     scale = 1.0 / (init_state.shape[0] * lax.axis_size(AXES))
-    chip = keep + shifted(send, "c", 1)
     members = slots * parts
-    received = lax.all_to_all(chip.reshape(members, -1, cols), RING, 0, 0, tiled=True)
+    other = shifted(send, "c", 1)
+    coded = encode(keep.reshape(members, -1, cols), other.reshape(members, -1, cols))
+    received = lax.all_to_all(coded, RING, 0, 0, tiled=True)
     spread, rest = sum_parts(received, slots, scale)
     own = lax.all_to_all(spread, ("y", "z"), 0, 0, tiled=True)
     other = shifted(own, "c", 1)

time: 120 us -> 105 us (0.88)
  blocking collectives: 42.7 us -> 37 us
  waiting for transfers between devices: 16.6 us -> 12.1 us
  local copies, waits for them, and re-layouts: 7.42 us -> 4.09 us
  Pallas kernels: 41.5 us -> 38.2 us
  other arithmetic: 2.44 us -> 4.27 us
    unnamed x17 -> x1, local copies, waits for them, and re-layouts: 6.76 us -> 0.99 us
    all_to_all x1, blocking collectives: 32.4 us -> 26.8 us  [on_device(): received = lax.all_to_all(coded, RING, 0, 0, tiled=True)]
    ppermute x5, waiting for transfers between devices: 16.6 us -> 12.1 us  [shifted(): lax.ppermute(array, axis, [(i, (i + by) % count) for i in range(count)])]
    pallas_call x1 -> x2, Pallas kernels: 39.9 us -> 36.1 us  [the longest x1 35.4 us: solve(): pl.pallas_call(series_kernel, name='series', out_shape=outs, in_specs=[ho...]
    concatenate x0 -> x1, local copies, waits for them, and re-layouts: none -> 1.66 us  [solve(): jnp.concatenate([init, b_out[None], prior[None], diff[None], ends, obs_st...]
    convert_element_type x0 -> x3, other arithmetic: none -> 1.36 us  [the longest x1 0.69 us: solve(): obs_steps.T.astype(F32).reshape(seen // 2, 2 * rows)]
  transfers between devices with their start and end apart: 5 -> 5, of which waited for: 5 -> 4; matrix products, arithmetic and copies ran while one was open for 2% -> 6% of each run, Pallas kernels for 0% -> 0%
where the time goes in v3:
time: 105 us; the launch traced here: 104 us
  Pallas kernels  38.2 us (36%)
  blocking collectives  37 us (35%)
  waiting for transfers between devices  12.1 us (12%)
  starting transfers between devices  8 us (8%)
  other arithmetic  4.27 us (4%)
  local copies, waits for them, and re-layouts  4.09 us (4%)
    pallas_call x1, Pallas kernels, solve(): pl.pallas_call(series_kernel, name='series', out_shape=outs, in_specs=[ho...  35.4 us
    all_to_all x1, blocking collectives, on_device(): received = lax.all_to_all(coded, RING, 0, 0, tiled=True)  26.8 us
    ppermute x5, waiting for transfers between devices, shifted(): lax.ppermute(array, axis, [(i, (i + by) % count) for i in range(count)])  12.1 us
    all_to_all x1, blocking collectives, on_device(): own = lax.all_to_all(spread, ('y', 'z'), 0, 0, tiled=True)  10.3 us
    ppermute x5, starting transfers between devices, shifted(): lax.ppermute(array, axis, [(i, (i + by) % count) for i in range(count)])  8 us
  transfers between devices with their start and end apart: 5, of which 4 were waited for; matrix products, arithmetic and copies ran while one was open for 6% of the time, Pallas kernels for 0%

profile of v3, /device:TPU:1, one launch (start us, length us, event | category | flops | bytes accessed | tf_op | source)
XLA Modules:
  0.0 104.3 jit_solution(6381894473558988977)
XLA Ops:
  0.6 0.7 broadcast_in_dim.22
  1.3 1.0 pad_maximum_fusion.piece_0
  2.3 3.4 %collective-permute-start.2 = (bf16[528,256]{1,0:T(8,128)(2,1)S(1)}, bf16[528,256]{1,0:T(8,128)(2,1)S(1)}, u32[]{:S(2)}, u32[]{:S(2)}) collective-permute-start(bf16[528,256]{1,0:T(8,128)(2,1)S(1)} %pad_maximum_fusion.piece_0), channel_id=1, source_target_pairs={{0,3},{1,0},{2,1},{3,2},{4,7},{5,4},{6,5},{7,6},{8,11},{9,8},{10,9... | collective-permute-start | bytes 811016 | tf_op jit(solution)/shard_map/ppermute | solution.py:419
  5.6 0.5 collective-permute-start.1
  6.2 0.6 collective-permute-start
  6.8 0.7 convert_element_type.12
  7.4 0.7 convert_bitcast_fusion
  8.1 0.8 fusion
  8.9 0.7 pad_maximum_fusion.1
  9.6 1.0 copy.23
  10.6 1.7 %concatenate.14.packed = f32[264,256]{1,0:T(8,128)S(1)} concatenate(f32[128,256]{1,0:T(8,128)} %param.13, f32[1,256]{1,0:T(1,128)} %bitcast.22, f32[1,256]{1,0:T(1,128)} %bitcast.23, f32[1,256]{1,0:T(1,128)} %bitcast.24, f32[1,256]{1,0:T(1,128)S(1)} %bitcast.21, f32[4,256]{1,0:T(4,128)S(1)} %reshape.35, f32[128,256]{1,0:T(8,128)S(1)} %maximum_convert_fusion), dimensions={0} | concatenate | bytes 540672 | tf_op jit(solution)/shard_map/concatenate | solution.py:248
  12.2 0.1 pad_add_fusion.place
  12.3 2.0 %collective-permute-done.1.piece_2 = bf16[528,256]{1,0:T(8,128)(2,1)S(1)} collective-permute-done((bf16[528,256]{1,0:T(8,128)(2,1)S(1)}, bf16[528,256]{1,0:T(8,128)(2,1)S(1)}, u32[]{:S(2)}, u32[]{:S(2)}) %collective-permute-start.1) | collective-permute-done | bytes 270368 | tf_op jit(solution)/shard_map/ppermute | solution.py:419
  14.3 7.1 %collective-permute-done.piece_1 = bf16[528,256]{1,0:T(8,128)(2,1)S(1)} collective-permute-done((bf16[528,256]{1,0:T(8,128)(2,1)S(1)}, bf16[528,256]{1,0:T(8,128)(2,1)S(1)}, u32[]{:S(2)}, u32[]{:S(2)}) %collective-permute-start) | collective-permute-done | bytes 270368 | tf_op jit(solution)/shard_map/ppermute | solution.py:419
  21.3 35.4 %series.1 = (f32[16,4,48,128]{3,2,1,0:T(8,128)S(1)}, f32[16,4,48,128]{3,2,1,0:T(8,128)S(1)}, f32[1,128]{1,0:T(1,128)}, f32[128,256]{1,0:T(8,128)}) custom-call(bf16[32,128,256]{2,1,0:T(8,128)(2,1)} %brown_home.1, f32[264,256]{1,0:T(8,128)S(1)} %concatenate.14.packed, bf16[8,128,128]{2,1,0:T(8,128)(2,1)S(1)} %bitcast.20, ...), custom_call_target="tpu_custom_call" | custom-call | flops 12884901888 | bytes 8388608 | tf_op jit(solution)/shard_map/series/pallas_call | solution.py:267
  56.8 0.6 collective-permute-start.3
  57.3 3.0 %collective-permute-done.3 = f32[16,4,48,128]{3,2,1,0:T(8,128)S(1)} collective-permute-done((f32[16,4,48,128]{3,2,1,0:T(8,128)S(1)}, f32[16,4,48,128]{3,2,1,0:T(8,128)S(1)}, u32[]{:S(2)}, u32[]{:S(2)}) %collective-permute-start.3) | collective-permute-done | bytes 1572896 | tf_op jit(solution)/shard_map/ppermute | solution.py:419
  60.4 0.7 encode.1
  61.1 26.8 %all_to_all.10.parts = s16[64,64,128]{2,1,0:T(8,128)(2,1)S(1)} all-to-all(s16[64,64,128]{2,1,0:T(8,128)(2,1)S(1)} %encode.1), channel_id=1, replica_groups=mesh['y'=4,'z'=4,'c'=2,'x'=4] {'y','z','x'}, dimensions={0} | all-to-all | bytes 2097152 | tf_op jit(solution)/shard_map/all_to_all | solution.py:467
  87.8 0.5 sum_parts.1
  88.4 10.3 %all_to_all.11.mine = f32[16,40,128]{2,1,0:T(8,128)S(1)} all-to-all(f32[16,40,128]{2,1,0:T(8,128)S(1)} %get-tuple-element.21), channel_id=1, replica_groups=mesh['y'=4,'z'=4,'c'=2,'x'=4] {'y','z'}, dimensions={0} | all-to-all | bytes 655360 | tf_op jit(solution)/shard_map/all_to_all | solution.py:469
  98.6 2.9 %collective-permute-start.4 = (f32[16,40,128]{2,1,0:T(8,128)S(1)}, f32[16,40,128]{2,1,0:T(8,128)S(1)}, u32[]{:S(2)}, u32[]{:S(2)}) collective-permute-start(f32[16,40,128]{2,1,0:T(8,128)S(1)} %all_to_all.11.mine), channel_id=1, source_target_pairs={{0,4},{4,0},{1,5},{5,1},{2,6},{6,2},{3,7},{7,3},{8,12},{12,8},{9,1... | collective-permute-start | bytes 983048 | tf_op jit(solution)/shard_map/ppermute | solution.py:419
  101.5 1.2 %slice_bitcast_fusion = (f32[256]{0:T(256)}, f32[256]{0:T(256)}, f32[2]{0:T(128)}) fusion(f32[8,128]{1,0:T(8,128)S(1)} %get-tuple-element.20), kind=kLoop, calls=%fused_computation.5 | loop fusion | flops 254 | bytes 5128 | tf_op jit(solution)/shard_map/reshape | solution.py:480
  102.8 1.5 %lay_out.1 = (f32[256,256]{1,0:T(8,128)}, f32[256,256]{1,0:T(8,128)}, f32[256,128]{1,0:T(8,128)}) custom-call(s32[2]{0:T(128)S(1)} %pad_add_fusion.place, f32[16,40,128]{2,1,0:T(8,128)S(1)} %all_to_all.11.mine, f32[16,40,128]{2,1,0:T(8,128)S(1)} %collective-permute-done.4.other), custom_call_target="tpu_custom_call" | custom-call | tf_op jit(solution)/shard_map/lay_out/pallas_call | solution.py:399
  (4 shorter events, 0.1 us)
Async XLA Ops:
  2.3 10.0 %collective-permute-start.2 = (bf16[528,256]{1,0:T(8,128)(2,1)S(1)}, bf16[528,256]{1,0:T(8,128)(2,1)S(1)}, u32[]{:S(2)}, u32[]{:S(2)}) collective-permute-start(bf16[528,256]{1,0:T(8,128)(2,1)S(1)} %pad_maximum_fusion.piece_0), channel_id=1, source_target_pairs={{0,3},{1,0},{2,1},{3,2},{4,7},{5,4},{6,5},{7,6},{8,11},{9,8},{10,9... | collective-permute-start | bytes 811016 | tf_op jit(solution)/shard_map/ppermute | solution.py:419
  5.6 8.6 %collective-permute-start.1 = (bf16[528,256]{1,0:T(8,128)(2,1)S(1)}, bf16[528,256]{1,0:T(8,128)(2,1)S(1)}, u32[]{:S(2)}, u32[]{:S(2)}) collective-permute-start(bf16[528,256]{1,0:T(8,128)(2,1)S(1)} %pad_maximum_fusion.piece_0), channel_id=1, source_target_pairs={{0,2},{1,3},{2,0},{3,1},{4,6},{5,7},{6,4},{7,5},{8,10},{9,11},{10,... | collective-permute-start | bytes 811016 | tf_op jit(solution)/shard_map/ppermute | solution.py:419
  6.2 15.2 %collective-permute-start = (bf16[528,256]{1,0:T(8,128)(2,1)S(1)}, bf16[528,256]{1,0:T(8,128)(2,1)S(1)}, u32[]{:S(2)}, u32[]{:S(2)}) collective-permute-start(bf16[528,256]{1,0:T(8,128)(2,1)S(1)} %pad_maximum_fusion.piece_0), channel_id=1, source_target_pairs={{0,1},{1,2},{2,3},{3,0},{4,5},{5,6},{6,7},{7,4},{8,9},{9,10},{10,1... | collective-permute-start | bytes 811016 | tf_op jit(solution)/shard_map/ppermute | solution.py:419
  56.8 3.6 %collective-permute-start.3 = (f32[16,4,48,128]{3,2,1,0:T(8,128)S(1)}, f32[16,4,48,128]{3,2,1,0:T(8,128)S(1)}, u32[]{:S(2)}, u32[]{:S(2)}) collective-permute-start(f32[16,4,48,128]{3,2,1,0:T(8,128)S(1)} %get-tuple-element.19), channel_id=1, source_target_pairs={{0,4},{4,0},{1,5},{5,1},{2,6},{6,2},{3,7},{7,3},{8,12},{12,8},{9,1... | collective-permute-start | bytes 4718600 | tf_op jit(solution)/shard_map/ppermute | solution.py:419
  98.6 4.2 %collective-permute-start.4 = (f32[16,40,128]{2,1,0:T(8,128)S(1)}, f32[16,40,128]{2,1,0:T(8,128)S(1)}, u32[]{:S(2)}, u32[]{:S(2)}) collective-permute-start(f32[16,40,128]{2,1,0:T(8,128)S(1)} %all_to_all.11.mine), channel_id=1, source_target_pairs={{0,4},{4,0},{1,5},{5,1},{2,6},{6,2},{3,7},{7,3},{8,12},{12,8},{9,1... | collective-permute-start | bytes 983048 | tf_op jit(solution)/shard_map/ppermute | solution.py:419

commit v4 on v3

--- a/solution.py
+++ b/solution.py
@@ -24,10 +24,14 @@
     brown_home,
     packed,
     obs,
-    piece_0,
-    piece_1,
-    piece_2,
-    piece_3,
+    half_0,
+    half_1,
+    half_2,
+    half_3,
+    rest_0,
+    rest_1,
+    rest_2,
+    rest_3,
     place,
     keep,
     send,
@@ -42,6 +46,7 @@
     upd_b,
     scaled,
     b_in,
+    w_in,
     w_out,
     w_in_t,
     w_out_t,
@@ -55,14 +60,18 @@
     acc_dec,
     brown,
     dec,
+    seen_now,
+    moved,
+    before,
     done,
 ):
     fetch = pltpu.make_async_copy(brown_home, brown, done)
     fetch.start()
     steps, rows, width = brown.shape
-    pieces = (piece_0, piece_1, piece_2, piece_3)
-    parts = len(pieces)
-    share = piece_0.shape[1]
+    halves = (half_0, half_1, half_2, half_3)
+    rests = (rest_0, rest_1, rest_2, rest_3)
+    parts = len(halves)
+    share = half_0.shape[1]
     hidden = parts * share
     cols = dec.shape[1]
     seen = obs.shape[0]
@@ -73,12 +82,21 @@
     dec[:rows, :] = dec_home[:, :cols]
     dec[rows:, :] = dec_home[:, cols:]
 
-    for q, piece in enumerate(pieces):
-        block = slice(q * share, (q + 1) * share)
-        w_out[block, :] = piece[width : width + share, :]
-        w_out_t[q] = jnp.transpose(piece[width : width + share, :])
-        w_in_t[block, :] = jnp.transpose(piece[:width, :])
-        b_in[:, block] = piece[width + share :, :].astype(F32)[:1]
+    core = place[0]
+
+    def unpack(ins, outs):
+        for q in range(parts):
+            block = slice(q * share, (q + 1) * share)
+            w_in[q] = ins[q][:width, :]
+            w_out[block, :] = outs[q][:width, :]
+            w_in_t[block, :] = jnp.transpose(ins[q][:width, :])
+            w_out_t[q] = jnp.transpose(outs[q][:width, :])
+
+    pl.when(core == 0)(lambda: unpack(halves, rests))
+    pl.when(core == 1)(lambda: unpack(rests, halves))
+    for q in range(parts):
+        b_in[:, q * share : (q + 1) * share] = halves[q][width:, :].astype(F32)[:1]
+
     step_b = column(step, rows)
     root_b = jnp.sqrt(step_b)
     lens_b = column(lens, rows)
@@ -98,48 +116,81 @@
     acc[...] = jnp.zeros_like(acc)
     acc_dec[...] = jnp.zeros_like(acc_dec)
 
-    def observe(k, low_now):
-        k_now = jnp.asarray(k, jnp.int32).astype(F32)
-        seen_now = jnp.dot(low_now, dec[...], preferred_element_type=F32)
-        total = jnp.zeros((rows, cols), F32)
-        squares = sq_acc[...]
-        for j in range(seen):
-            misfit = jnp.where(obs_at[j] == k_now, seen_now - obs[j].astype(F32), 0.0)
+    early = 4
+    seen_now[...] = jnp.zeros_like(seen_now)
+    moved[...] = jnp.broadcast_to(-b_out, (rows, width))
+    before[...] = jnp.zeros_like(before)
+
+    def observe_some(k, which, total, squares):
+        stamp = k.astype(F32)
+        product = seen_now[...]
+        for j in which:
+            misfit = jnp.where(obs_at[j] == stamp, product - obs[j].astype(F32), 0.0)
             squares = squares + misfit * misfit
             total = total + misfit.astype(BF16).astype(F32)
+        return total, squares
+
+    def store_back(total, at):
+        high = total.astype(BF16)
+        seen_back[at, :, :cols] = high
+        seen_back[at, :, cols:] = (total - high.astype(F32)).astype(BF16)
+
+    def observe(k, at):
+        total, squares = observe_some(k, range(seen), jnp.zeros((rows, cols), F32), sq_acc[...])
         sq_acc[...] = squares
-        high = total.astype(BF16)
-        seen_back[k, :, :cols] = high
-        seen_back[k, :, cols:] = (total - high.astype(F32)).astype(BF16)
+        store_back(total, at)
+
+    def settle(k):
+        at = jnp.maximum(k, 0)
+        factor = wide(jnp.where(k.astype(F32) < lens_b, step_b, 0.0))
+        residual = (moved[...] + b_out + prior * before[...]) * inv
+        scaled[at] = residual * inv
+        spent = factor * (residual * residual)
+        kl_acc[...] += spent[:, :rows] + spent[:, rows:]
 
     def forward(k, _):
         now = state[...]
         low_now = now.astype(BF16)
         low[k] = low_now
-        for q in range(parts):
-            block = slice(q * share, (q + 1) * share)
-            pre = jnp.dot(low_now, pieces[q][:width, :], preferred_element_type=F32) + b_in[:, block]
-            act[k, :, block] = jnp.tanh(pre).astype(BF16)
-        observe(k, low_now)
-        drift = (
-            jnp.dot(act[k], w_out[...], preferred_element_type=F32)
-            + b_out
-        )
         live = k.astype(F32) < lens_b
         factor = wide(jnp.where(live, step_b, 0.0))
         noise = wide(jnp.where(live, root_b, 0.0))
-        residual = (drift + prior * now) * inv
-        scaled[k] = residual * inv
-        spent = factor * (residual * residual)
-        kl_acc[...] += spent[:, :rows] + spent[:, rows:]
-        state[...] = now + (factor * drift + diff * noise * brown[k].astype(F32))
+        base = now + (factor * b_out + diff * noise * brown[k].astype(F32))
+        past = k - 1
+        total, squares = observe_some(
+            past, range(early), jnp.zeros((rows, cols), F32), sq_acc[...]
+        )
+        floor = jnp.min((squares + jnp.abs(total)).reshape(rows // 8, 8, cols), axis=0)
+        nothing = wide(jnp.minimum(floor, 0.0))[None]
+        for q in range(parts):
+            block = slice(q * share, (q + 1) * share)
+            pre = jnp.dot(low_now, w_in[q], preferred_element_type=F32)
+            if q == 0:
+                pre = (pre.reshape(rows // 8, 8, share) + (nothing + b_in[:, block])).reshape(
+                    rows, share
+                )
+            else:
+                pre = pre + b_in[:, block]
+            act[k, :, block] = jnp.tanh(pre).astype(BF16)
+        settle(past)
+        total, squares = observe_some(past, range(early, seen), total, squares)
+        sq_acc[...] = squares
+        store_back(total, jnp.maximum(past, 0))
+        seen_now[...] = jnp.dot(low_now, dec[...], preferred_element_type=F32)
+        product = jnp.dot(act[k], w_out[...], preferred_element_type=F32)
+        moved[...] = product
+        before[...] = now
+        state[...] = base + factor * product
         return 0
 
     fetch.wait()
     lax.fori_loop(0, steps, forward, 0)
+    settle(jnp.int32(steps - 1))
+    observe(jnp.int32(steps - 1), steps - 1)
     last = state[...].astype(BF16)
     low[steps] = last
-    observe(steps, last)
+    seen_now[...] = jnp.dot(last, dec[...], preferred_element_type=F32)
+    observe(jnp.int32(steps), steps)
 
     state[...] = jnp.dot(
         seen_back[steps], w_in_t[hidden:, :], preferred_element_type=F32
@@ -202,11 +253,10 @@
     final = acc_dec[...] + lax.dot_general(
         low[steps], seen_back[steps], turned, preferred_element_type=F32
     )
-    core = place[0]
     spot = place[1]
     slots = keep.shape[0]
     deep = width // slots
-    halves = share // cols
+    lanes = share // cols
     acc_dec[:, :cols] = final[:, :cols] + final[:, cols:]
     in_sum = jnp.sum(in_acc[...], axis=0, keepdims=True)
     out_sum = jnp.sum(out_acc[...], axis=0, keepdims=True)
@@ -214,16 +264,16 @@
     loglik = -0.5 * jnp.sum(jnp.transpose(sq_acc[...]), axis=0, keepdims=True)
     rest = [out_sum[:, p * cols : (p + 1) * cols] for p in range(width // cols)]
     rest = rest + [loglik, kl]
-    rest = rest + [jnp.zeros((8 - halves - len(rest), cols), F32)]
-    base = halves * deep
+    rest = rest + [jnp.zeros((8 - lanes - len(rest), cols), F32)]
+    base = lanes * deep
     tile = slots * 8
     for half, out in ((core, keep), (1 - core, send)):
         decs = acc_dec[pl.ds(pl.multiple_of(half * tile, 8), tile), :cols].reshape(slots, 8, cols)
         for s in range(parts):
             q = lax.rem(spot + (parts - s), parts)
-            aux = [in_sum[:, s * share + p * cols : s * share + (p + 1) * cols] for p in range(halves)]
+            aux = [in_sum[:, s * share + p * cols : s * share + (p + 1) * cols] for p in range(lanes)]
             aux = jnp.concatenate(aux + rest, axis=0)
-            for p in range(halves):
+            for p in range(lanes):
                 block = slice(s * share + p * cols, s * share + (p + 1) * cols)
                 out[:, q, p * deep : (p + 1) * deep, :] = acc[half, :, block].reshape(
                     slots, deep, cols
@@ -234,11 +284,11 @@
     elbo[...] = (loglik - kl) / divisor
 
 
-def solve(init, brown, step, lengths, obs_steps, observed, pieces, b_out, dec, prior, diff, place, slots):
+def solve(init, brown, step, lengths, obs_steps, observed, halves, rests, b_out, dec, prior, diff, place, slots):
     rows, width = init.shape
     steps = brown.shape[0]
-    parts = len(pieces)
-    share = pieces[0].shape[1]
+    parts = len(halves)
+    share = halves[0].shape[1]
     hidden = parts * share
     seen, cols = observed.shape[1:]
     vmem = pl.BlockSpec(memory_space=pltpu.VMEM)
@@ -269,7 +319,7 @@
         name="series",
         out_shape=outs,
         in_specs=[home]
-        + [vmem] * (2 + parts)
+        + [vmem] * (2 + 2 * parts)
         + [pl.BlockSpec(memory_space=pltpu.SMEM)],
         out_specs=(vmem,) * len(outs),
         scratch_shapes=[
@@ -282,6 +332,7 @@
             pltpu.VMEM((2, rows, width), BF16),
             pltpu.VMEM((steps, rows, width), F32),
             pltpu.VMEM((1, hidden), F32),
+            pltpu.VMEM((parts, width, share), BF16),
             pltpu.VMEM((hidden, width), BF16),
             pltpu.VMEM((hidden + 2 * cols, width), BF16),
             pltpu.VMEM((parts, width, share), BF16),
@@ -295,6 +346,9 @@
             pltpu.VMEM((width, 2 * cols), F32),
             pltpu.VMEM((steps, rows, width), BF16),
             pltpu.VMEM((width, cols), BF16),
+            pltpu.VMEM((rows, cols), F32),
+            pltpu.VMEM((rows, width), F32),
+            pltpu.VMEM((rows, width), F32),
             pltpu.SemaphoreType.DMA,
         ],
         compiler_params=pltpu.CompilerParams(vmem_limit_bytes=48 * 1024 * 1024),
@@ -307,7 +361,8 @@
         brown,
         packed,
         jnp.transpose(observed, (1, 0, 2)),
-        *pieces,
+        *halves,
+        *rests,
         place,
     )
 
@@ -442,8 +497,10 @@
     core = lax.axis_index("c")
     spot = lax.axis_index("x")
 
-    mine = jnp.concatenate([w_in, w_out, jnp.broadcast_to(b_in[None], (16, share))], axis=0)
-    pieces = [mine] + [shifted(mine, "x", by) for by in range(1, parts)]
+    bias_rows = jnp.broadcast_to(b_in[None], (16, share))
+    half = jnp.concatenate([jnp.where(core == 0, w_in, w_out), bias_rows], axis=0)
+    halves = [half] + [shifted(half, "x", by) for by in range(1, parts)]
+    rests = [jnp.where(core == 0, w_out, w_in)] + [shifted(got, "c", 1) for got in halves[1:]]
     place = jnp.stack([core, spot]).astype(jnp.int32)
     keep, send, elbo, grad_init = solve(
         init_state,
@@ -452,7 +509,8 @@
         lengths,
         obs_steps,
         observed,
-        pieces,
+        halves,
+        rests,
         b_out,
         decoder,
         prior_rate,

time: 105 us -> 99.7 us (0.950)
  waiting for transfers between devices: 12.1 us -> 6.55 us
  starting transfers between devices: 8 us -> 11.2 us
  Pallas kernels: 38.2 us -> 36.3 us
  local copies, waits for them, and re-layouts: 4.09 us -> 2.49 us
    ppermute x5 -> x8, waiting for transfers between devices: 12.1 us -> 6.55 us  [shifted(): lax.ppermute(array, axis, [(i, (i + by) % count) for i in range(count)])]
    ppermute x5 -> x8, starting transfers between devices: 8 us -> 11.2 us  [shifted(): lax.ppermute(array, axis, [(i, (i + by) % count) for i in range(count)])]
    pallas_call x1, Pallas kernels: 35.4 us -> 33.6 us  [solve(): pl.pallas_call(series_kernel, name='series', out_shape=outs, in_specs=[ho...]
    concatenate x1, local copies, waits for them, and re-layouts: 1.66 us -> 0.04 us  [solve(): jnp.concatenate([init, b_out[None], prior[None], diff[None], ends, obs_st...]
  transfers between devices with their start and end apart: 5 -> 8, of which waited for: 4 -> 4; matrix products, arithmetic and copies ran while one was open for 6% -> 5% of each run, Pallas kernels for 0% -> 0%
where the time goes in v4:
time: 99.7 us; the launch traced here: 99.3 us
  blocking collectives  37.6 us (38%)
  Pallas kernels  36.3 us (36%)
  starting transfers between devices  11.2 us (11%)
  waiting for transfers between devices  6.55 us (7%)
  other arithmetic  4.34 us (4%)
  local copies, waits for them, and re-layouts  2.49 us (2%)
    pallas_call x1, Pallas kernels, solve(): pl.pallas_call(series_kernel, name='series', out_shape=outs, in_specs=[ho...  33.6 us
    all_to_all x1, blocking collectives, on_device(): received = lax.all_to_all(coded, RING, 0, 0, tiled=True)  27.1 us
    ppermute x8, starting transfers between devices, shifted(): lax.ppermute(array, axis, [(i, (i + by) % count) for i in range(count)])  11.2 us
    all_to_all x1, blocking collectives, on_device(): own = lax.all_to_all(spread, ('y', 'z'), 0, 0, tiled=True)  10.5 us
    ppermute x8, waiting for transfers between devices, shifted(): lax.ppermute(array, axis, [(i, (i + by) % count) for i in range(count)])  6.55 us
  transfers between devices with their start and end apart: 8, of which 4 were waited for; matrix products, arithmetic and copies ran while one was open for 5% of the time, Pallas kernels for 0%

profile of v4, /device:TPU:1, one launch (start us, length us, event | category | flops | bytes accessed | tf_op | source)
XLA Modules:
  0.0 99.3 jit_solution(117833402503586914)
XLA Ops:
  0.7 1.0 %broadcast_select_fusion = (bf16[256,256]{1,0:T(8,128)(2,1)S(1)}, bf16[256,256]{1,0:T(8,128)(2,1)S(1)}) fusion(bf16[256,256]{1,0:T(8,128)(2,1)} %param.21, bf16[256,256]{1,0:T(8,128)(2,1)} %param.19, pred[]{:T(512)S(6)} %eq.4), kind=kLoop, calls=%fused_computation.2 | loop fusion | flops 131072 | bytes 524289 | tf_op jit(solution)/shard_map/jit(_where)/select_n | solution.py:503
  1.7 0.7 broadcast_in_dim.22
  2.4 3.4 %collective-permute-start.2 = (bf16[272,256]{1,0:T(8,128)(2,1)S(1)}, bf16[272,256]{1,0:T(8,128)(2,1)S(1)}, u32[]{:S(2)}, u32[]{:S(2)}) collective-permute-start(bf16[272,256]{1,0:T(8,128)(2,1)S(1)} %pad_maximum_fusion.half_0), channel_id=1, source_target_pairs={{0,3},{1,0},{2,1},{3,2},{4,7},{5,4},{6,5},{7,6},{8,11},{9,8},{10,9... | collective-permute-start | bytes 417800 | tf_op jit(solution)/shard_map/ppermute | solution.py:474
  5.8 0.5 collective-permute-start.1
  6.3 0.6 collective-permute-start
  6.9 0.8 fusion
  7.7 0.7 convert_bitcast_fusion
  8.4 0.7 convert_element_type.12
  9.0 2.1 %collective-permute-done.2.half_3 = bf16[272,256]{1,0:T(8,128)(2,1)S(1)} collective-permute-done((bf16[272,256]{1,0:T(8,128)(2,1)S(1)}, bf16[272,256]{1,0:T(8,128)(2,1)S(1)}, u32[]{:S(2)}, u32[]{:S(2)}) %collective-permute-start.2) | collective-permute-done | bytes 139296 | tf_op jit(solution)/shard_map/ppermute | solution.py:474
  11.1 1.5 %collective-permute-start.5 = (bf16[272,256]{1,0:T(8,128)(2,1)S(1)}, bf16[272,256]{1,0:T(8,128)(2,1)S(1)}, u32[]{:S(2)}, u32[]{:S(2)}) collective-permute-start(bf16[272,256]{1,0:T(8,128)(2,1)S(1)} %collective-permute-done.2.half_3), channel_id=1, source_target_pairs={{0,4},{4,0},{1,5},{5,1},{2,6},{6,2},{3,7},{7,3},{8,12},{12,8},{9,1... | collective-permute-start | bytes 417800 | tf_op jit(solution)/shard_map/ppermute | solution.py:474
  12.6 2.1 %collective-permute-start.4 = (bf16[272,256]{1,0:T(8,128)(2,1)S(1)}, bf16[272,256]{1,0:T(8,128)(2,1)S(1)}, u32[]{:S(2)}, u32[]{:S(2)}) collective-permute-start(bf16[272,256]{1,0:T(8,128)(2,1)S(1)} %collective-permute-done.1.half_2), channel_id=1, source_target_pairs={{0,4},{4,0},{1,5},{5,1},{2,6},{6,2},{3,7},{7,3},{8,12},{12,8},{9,1... | collective-permute-start | bytes 417800 | tf_op jit(solution)/shard_map/ppermute | solution.py:474
  14.8 1.0 %collective-permute-done.half_1 = bf16[272,256]{1,0:T(8,128)(2,1)S(1)} collective-permute-done((bf16[272,256]{1,0:T(8,128)(2,1)S(1)}, bf16[272,256]{1,0:T(8,128)(2,1)S(1)}, u32[]{:S(2)}, u32[]{:S(2)}) %collective-permute-start) | collective-permute-done | bytes 139296 | tf_op jit(solution)/shard_map/ppermute | solution.py:474
  15.8 0.6 collective-permute-start.3
  16.3 0.7 pad_maximum_fusion.1
  17.0 1.0 copy.23
  18.2 33.6 %series.1 = (f32[16,4,48,128]{3,2,1,0:T(8,128)S(1)}, f32[16,4,48,128]{3,2,1,0:T(8,128)S(1)}, f32[1,128]{1,0:T(1,128)}, f32[128,256]{1,0:T(8,128)}) custom-call(bf16[32,128,256]{2,1,0:T(8,128)(2,1)} %brown_home.1, f32[264,256]{1,0:T(8,128)S(1)} %concatenate.14.packed, bf16[8,128,128]{2,1,0:T(8,128)(2,1)S(1)} %bitcast.20, ...), custom_call_target="tpu_custom_call" | custom-call | flops 12884901888 | bytes 8388608 | tf_op jit(solution)/shard_map/series/pallas_call | solution.py:317
  51.9 3.4 %collective-permute-done.6 = f32[16,4,48,128]{3,2,1,0:T(8,128)S(1)} collective-permute-done((f32[16,4,48,128]{3,2,1,0:T(8,128)S(1)}, f32[16,4,48,128]{3,2,1,0:T(8,128)S(1)}, u32[]{:S(2)}, u32[]{:S(2)}) %collective-permute-start.6) | collective-permute-done | bytes 1572896 | tf_op jit(solution)/shard_map/ppermute | solution.py:474
  55.3 0.7 encode.1
  55.9 27.1 %all_to_all.10.parts = s16[64,64,128]{2,1,0:T(8,128)(2,1)S(1)} all-to-all(s16[64,64,128]{2,1,0:T(8,128)(2,1)S(1)} %encode.1), channel_id=1, replica_groups=mesh['y'=4,'z'=4,'c'=2,'x'=4] {'y','z','x'}, dimensions={0} | all-to-all | bytes 2097152 | tf_op jit(solution)/shard_map/all_to_all | solution.py:525
  83.1 0.5 sum_parts.1
  83.6 10.5 %all_to_all.11.mine = f32[16,40,128]{2,1,0:T(8,128)S(1)} all-to-all(f32[16,40,128]{2,1,0:T(8,128)S(1)} %get-tuple-element.21), channel_id=1, replica_groups=mesh['y'=4,'z'=4,'c'=2,'x'=4] {'y','z'}, dimensions={0} | all-to-all | bytes 655360 | tf_op jit(solution)/shard_map/all_to_all | solution.py:527
  94.1 2.4 %collective-permute-start.7 = (f32[16,40,128]{2,1,0:T(8,128)S(1)}, f32[16,40,128]{2,1,0:T(8,128)S(1)}, u32[]{:S(2)}, u32[]{:S(2)}) collective-permute-start(f32[16,40,128]{2,1,0:T(8,128)S(1)} %all_to_all.11.mine), channel_id=1, source_target_pairs={{0,4},{4,0},{1,5},{5,1},{2,6},{6,2},{3,7},{7,3},{8,12},{12,8},{9,1... | collective-permute-start | bytes 983048 | tf_op jit(solution)/shard_map/ppermute | solution.py:474
  96.5 1.2 %slice_bitcast_fusion = (f32[256]{0:T(256)}, f32[256]{0:T(256)}, f32[2]{0:T(128)}) fusion(f32[8,128]{1,0:T(8,128)S(1)} %get-tuple-element.20), kind=kLoop, calls=%fused_computation.7 | loop fusion | flops 254 | bytes 5128 | tf_op jit(solution)/shard_map/reshape | solution.py:538
  97.8 1.5 %lay_out.1 = (f32[256,256]{1,0:T(8,128)}, f32[256,256]{1,0:T(8,128)}, f32[256,128]{1,0:T(8,128)}) custom-call(s32[2]{0:T(128)S(1)} %pad_add_fusion.place, f32[16,40,128]{2,1,0:T(8,128)S(1)} %all_to_all.11.mine, f32[16,40,128]{2,1,0:T(8,128)S(1)} %collective-permute-done.7.other), custom_call_target="tpu_custom_call" | custom-call | tf_op jit(solution)/shard_map/lay_out/pallas_call | solution.py:454
  (19 shorter events, 0.3 us)
Async XLA Ops:
  0.6 17.4 %copy-start.3 = (f32[256]{0:T(256)S(1)}, f32[256]{0:T(256)}, u32[]{:S(2)}) copy-start(f32[256]{0:T(256)} %param.25) | copy-start | bytes 3076
  0.6 17.4 %copy-start.2 = (f32[256]{0:T(256)S(1)}, f32[256]{0:T(256)}, u32[]{:S(2)}) copy-start(f32[256]{0:T(256)} %param.24) | copy-start | bytes 3076
  0.7 17.4 %copy-start.1 = (f32[256]{0:T(256)S(1)}, f32[256]{0:T(256)}, u32[]{:S(2)}) copy-start(f32[256]{0:T(256)} %param.22) | copy-start | bytes 3076
  0.7 17.4 %copy-start = (f32[128,256]{1,0:T(8,128)S(1)}, f32[128,256]{1,0:T(8,128)}, u32[]{:S(2)}) copy-start(f32[128,256]{1,0:T(8,128)} %param.13) | copy-start | bytes 393220
  2.4 8.7 %collective-permute-start.2 = (bf16[272,256]{1,0:T(8,128)(2,1)S(1)}, bf16[272,256]{1,0:T(8,128)(2,1)S(1)}, u32[]{:S(2)}, u32[]{:S(2)}) collective-permute-start(bf16[272,256]{1,0:T(8,128)(2,1)S(1)} %pad_maximum_fusion.half_0), channel_id=1, source_target_pairs={{0,3},{1,0},{2,1},{3,2},{4,7},{5,4},{6,5},{7,6},{8,11},{9,8},{10,9... | collective-permute-start | bytes 417800 | tf_op jit(solution)/shard_map/ppermute | solution.py:474
  5.8 6.9 %collective-permute-start.1 = (bf16[272,256]{1,0:T(8,128)(2,1)S(1)}, bf16[272,256]{1,0:T(8,128)(2,1)S(1)}, u32[]{:S(2)}, u32[]{:S(2)}) collective-permute-start(bf16[272,256]{1,0:T(8,128)(2,1)S(1)} %pad_maximum_fusion.half_0), channel_id=1, source_target_pairs={{0,2},{1,3},{2,0},{3,1},{4,6},{5,7},{6,4},{7,5},{8,10},{9,11},{10,... | collective-permute-start | bytes 417800 | tf_op jit(solution)/shard_map/ppermute | solution.py:474
  6.3 9.5 %collective-permute-start = (bf16[272,256]{1,0:T(8,128)(2,1)S(1)}, bf16[272,256]{1,0:T(8,128)(2,1)S(1)}, u32[]{:S(2)}, u32[]{:S(2)}) collective-permute-start(bf16[272,256]{1,0:T(8,128)(2,1)S(1)} %pad_maximum_fusion.half_0), channel_id=1, source_target_pairs={{0,1},{1,2},{2,3},{3,0},{4,5},{5,6},{6,7},{7,4},{8,9},{9,10},{10,1... | collective-permute-start | bytes 417800 | tf_op jit(solution)/shard_map/ppermute | solution.py:474
  11.1 7.1 %collective-permute-start.5 = (bf16[272,256]{1,0:T(8,128)(2,1)S(1)}, bf16[272,256]{1,0:T(8,128)(2,1)S(1)}, u32[]{:S(2)}, u32[]{:S(2)}) collective-permute-start(bf16[272,256]{1,0:T(8,128)(2,1)S(1)} %collective-permute-done.2.half_3), channel_id=1, source_target_pairs={{0,4},{4,0},{1,5},{5,1},{2,6},{6,2},{3,7},{7,3},{8,12},{12,8},{9,1... | collective-permute-start | bytes 417800 | tf_op jit(solution)/shard_map/ppermute | solution.py:474
  12.6 5.5 %collective-permute-start.4 = (bf16[272,256]{1,0:T(8,128)(2,1)S(1)}, bf16[272,256]{1,0:T(8,128)(2,1)S(1)}, u32[]{:S(2)}, u32[]{:S(2)}) collective-permute-start(bf16[272,256]{1,0:T(8,128)(2,1)S(1)} %collective-permute-done.1.half_2), channel_id=1, source_target_pairs={{0,4},{4,0},{1,5},{5,1},{2,6},{6,2},{3,7},{7,3},{8,12},{12,8},{9,1... | collective-permute-start | bytes 417800 | tf_op jit(solution)/shard_map/ppermute | solution.py:474
  15.8 2.4 %collective-permute-start.3 = (bf16[272,256]{1,0:T(8,128)(2,1)S(1)}, bf16[272,256]{1,0:T(8,128)(2,1)S(1)}, u32[]{:S(2)}, u32[]{:S(2)}) collective-permute-start(bf16[272,256]{1,0:T(8,128)(2,1)S(1)} %collective-permute-done.half_1), channel_id=1, source_target_pairs={{0,4},{4,0},{1,5},{5,1},{2,6},{6,2},{3,7},{7,3},{8,12},{12,8},{9,1... | collective-permute-start | bytes 417800 | tf_op jit(solution)/shard_map/ppermute | solution.py:474
  51.8 3.5 %collective-permute-start.6 = (f32[16,4,48,128]{3,2,1,0:T(8,128)S(1)}, f32[16,4,48,128]{3,2,1,0:T(8,128)S(1)}, u32[]{:S(2)}, u32[]{:S(2)}) collective-permute-start(f32[16,4,48,128]{3,2,1,0:T(8,128)S(1)} %get-tuple-element.19), channel_id=1, source_target_pairs={{0,4},{4,0},{1,5},{5,1},{2,6},{6,2},{3,7},{7,3},{8,12},{12,8},{9,1... | collective-permute-start | bytes 4718600 | tf_op jit(solution)/shard_map/ppermute | solution.py:474
  94.1 3.7 %collective-permute-start.7 = (f32[16,40,128]{2,1,0:T(8,128)S(1)}, f32[16,40,128]{2,1,0:T(8,128)S(1)}, u32[]{:S(2)}, u32[]{:S(2)}) collective-permute-start(f32[16,40,128]{2,1,0:T(8,128)S(1)} %all_to_all.11.mine), channel_id=1, source_target_pairs={{0,4},{4,0},{1,5},{5,1},{2,6},{6,2},{3,7},{7,3},{8,12},{12,8},{9,1... | collective-permute-start | bytes 983048 | tf_op jit(solution)/shard_map/ppermute | solution.py:474
